TPU v7x, 32 devices: a whole 2x2x4 slice. The times are simulated.
32 devices in a mesh: pix: 32 (over z, y, x, core).
Axes of the slice: x: 2, y: 2, z: 4, core: 2. Of those that a mesh axis runs over, the one named last changes fastest.
Arguments:
- green: float32 [2048, 6144], P('pix'), may hold values from -200 to 200, as said below
- sketch: float32 [6144, 128], P('pix'), may hold values from -0.078125 to 0.078125
Outputs:
- basis: float32 [2048, 128], P('pix')
- projection: float32 [6144, 128], P('pix')
- spectrum_gram: float32 [128, 128], replicated
Inputs may be any that keep to these rules, and one draw needn't show every extreme that they name: `green`: finite real entries; each patch's column has its own scale.
All inputs are finite; a program needn't handle non-finite values.
Results may differ from a plain program's by a relative error of at most 0.000086.
Values sent between devices are 32-bit elements; how exact they have to be, the bound alone decides.
A program may use at most 64 MiB of HBM per device.

v0:
```python
import functools

import jax
import jax.numpy as jnp
from jax import lax
from jax.experimental import pallas as pl
from jax.experimental.pallas import tpu as pltpu
from jax.sharding import PartitionSpec as P

MESH = pl.DeviceIdType.MESH
F32 = jnp.float32
BF16 = jnp.bfloat16
PANEL = 8


def grid_of(devices):
    cores = 2 if devices % 2 == 0 else 1
    chips = devices // cores
    side = 1
    for k in range(1, chips + 1):
        if chips % (k * k) == 0 and k * k * k <= chips:
            side = k
    return cores, side, side, chips // (side * side)


def split(v):
    hi = v.astype(BF16)
    return hi, (v - hi.astype(F32)).astype(BF16)


def thirds(v):
    a = v.astype(BF16).astype(F32)
    b = (v - a).astype(BF16).astype(F32)
    return a, b, v - a - b


def dot(a, b, dims=((1,), (0,))):
    return lax.dot_general(a, b, (dims, ((), ())), preferred_element_type=F32)


def exact(a, b, dims=((1,), (0,))):
    return lax.dot_general(
        a, b, (dims, ((), ())), precision=lax.Precision.HIGHEST, preferred_element_type=F32
    )


def kernel(grid, total_pixels, green_in, sketch_in, basis, projection, inverse_out, spec, scratch):
    C, X, Y, Z = grid
    assert C == 2
    r = scratch
    me = lax.axis_index("pix")
    c = lax.rem(me, C)
    x = lax.rem(me // C, X)
    y = lax.rem(me // (C * X), Y)
    z = me // (C * X * Y)
    green, sketch = r["green"], r["sketch"]
    load_sketch = pltpu.make_async_copy(sketch_in, sketch, r["load"].at[0])
    load_green = pltpu.make_async_copy(green_in, green, r["load"].at[1])
    load_sketch.start()
    load_green.start()
    rows = sketch.shape[0]
    rank = sketch.shape[1]
    pixels = green.shape[0]
    half_a = (rows // 2 + 7) // 8 * 8
    part_a, part_b = pl.ds(0, half_a), pl.ds(half_a, rows - half_a)
    slab = X * Y * C * rows

    def dev(zz, yy, xx, cc):
        return (((zz * Y + yy) * X + xx) * C + cc,)

    def at(v, d, n):
        return lax.rem(v + d + n, n)

    partner = dev(z, y, x, 1 - c)
    counter = [0]
    sends = []

    def copy(src, dst, recv, to):
        d = pltpu.make_async_remote_copy(
            src_ref=src, dst_ref=dst, send_sem=r["send"].at[counter[0]], recv_sem=recv,
            device_id=to, device_id_type=MESH,
        )
        counter[0] += 1
        sends.append(d)
        d.start()

    def arrive(dst, recv):
        pltpu.make_async_remote_copy(
            src_ref=dst, dst_ref=dst, send_sem=r["send"].at[0], recv_sem=recv,
            device_id=partner, device_id_type=MESH,
        ).wait_recv()

    barrier = pltpu.get_barrier_semaphore()
    plane = [(dy, dx) for dy in range(Y) for dx in range(X) if (dy, dx) != (0, 0)]
    peers = [partner]
    peers += [dev(z, at(y, dy, Y), at(x, dx, X), c) for dy, dx in plane]
    peers += [dev(at(z, d, Z), y, x, c) for d in range(1, Z)]
    for peer in peers:
        pl.semaphore_signal(barrier, inc=1, device_id=peer, device_id_type=MESH)
    load_sketch.wait()
    pl.semaphore_wait(barrier, len(peers))

    short = jnp.minimum(z, Z - 1 - z)
    side = jnp.where(z <= Z - 1 - z, 1, -1)

    def near(p):
        sign = side if p % 2 else -side
        return z + jnp.where(p <= 2 * short, sign * ((p + 1) // 2), side * (p - short))

    others = range(1, Z)

    gat = r["gat"]

    def ag1(s):
        zc = near(s)
        if s == 0:
            mine_a, mine_b = sketch.at[part_a], sketch.at[part_b]
        else:
            arrive(gat.at[zc, y, x, c], r["agz"].at[zc])
            mine_a, mine_b = gat.at[zc, y, x, c, part_a], gat.at[zc, y, x, c, part_b]
        for dx in range(1, X):
            copy(mine_a, gat.at[zc, y, x, c, part_a], r["agxa"].at[s, dx],
                 dev(z, y, at(x, dx, X), c))
        for dy in range(1, Y):
            copy(mine_b, gat.at[zc, y, x, c, part_b], r["agyb"].at[s, dy],
                 dev(z, at(y, dy, Y), x, c))
        if s == 0:
            for p in others:
                copy(sketch, gat.at[z, y, x, c], r["agz"].at[z], dev(near(p), y, x, c))
            gat[z, y, x, c] = sketch[...]

    def ag2(s):
        zc = near(s)
        for dx in range(1, X):
            arrive(gat.at[zc, y, at(x, -dx, X), c, part_a], r["agxa"].at[s, dx])
        for dy in range(1, Y):
            ref = gat.at[zc, y, :, c, part_a]
            copy(ref, ref, r["agya"].at[s, dy], dev(z, at(y, dy, Y), x, c))
        for dy in range(1, Y):
            arrive(gat.at[zc, at(y, -dy, Y), x, c, part_b], r["agyb"].at[s, dy])
        for dx in range(1, X):
            ref = gat.at[zc, :, x, c, part_b]
            copy(ref, ref, r["agxb"].at[s, dx], dev(z, y, at(x, dx, X), c))

    def ag3(s):
        zc = near(s)
        for dy in range(1, Y):
            arrive(gat.at[zc, at(y, -dy, Y), :, c, part_a], r["agya"].at[s, dy])
        for dx in range(1, X):
            arrive(gat.at[zc, :, at(x, -dx, X), c, part_b], r["agxb"].at[s, dx])
        ref = gat.at[zc, :, :, c]
        copy(ref, ref, r["agd"].at[s], partner)

    def ag4(s):
        zc = near(s)
        arrive(gat.at[zc, :, :, 1 - c], r["agd"].at[s])
        if s == 0:
            load_green.wait()
        block = gat[zc].reshape(slab, rank)
        g = green[:, pl.ds(pl.multiple_of(zc * slab, 128), slab)]
        g_hi, g_lo = split(g)
        b_hi, b_lo = split(block)
        both = dot(jnp.concatenate([g_hi, g_lo], axis=0), b_hi)
        out = both[:pixels] + both[pixels:] + dot(g_hi, b_lo)
        if s == 0:
            r["sketched"][...] = out
        else:
            r["sketched"][...] += out

    def pipeline(stages, items, extra):
        for t in range(len(items) + len(stages) - 1):
            for k, stage in enumerate(stages):
                if 0 <= t - k < len(items):
                    stage(items[t - k])
            for job in extra.get(t, ()):
                job()

    pipeline([ag1, ag2, ag3, ag4], range(Z), {})
    sketched = r["sketched"][...]
    s_hi, s_lo = split(sketched)
    packed = jnp.concatenate([s_hi, s_lo, s_hi, s_lo], axis=0)

    def all_sum(k, value, out):
        inc, mid, top = r["ar_in"].at[k], r["ar_mid"].at[k], r["ar_top"].at[k]
        h = rank // C
        keep = pl.ds(pl.multiple_of(c * h, h), h)
        give = pl.ds(pl.multiple_of((1 - c) * h, h), h)
        here = y * X + x

        def step0():
            r["ar_src"][k] = value()
            copy(r["ar_src"].at[k, give], inc, r["ar0"].at[k], partner)

        def step1():
            arrive(inc, r["ar0"].at[k])
            mid[here] = r["ar_src"][k, keep] + inc[...]
            for i, (dy, dx) in enumerate(plane):
                copy(mid.at[here], mid.at[here], r["ar1"].at[k, i],
                     dev(z, at(y, dy, Y), at(x, dx, X), c))

        def step2():
            for i, (dy, dx) in enumerate(plane):
                arrive(mid.at[at(y, -dy, Y) * X + at(x, -dx, X)], r["ar1"].at[k, i])
            top[z] = jnp.sum(mid[...], axis=0)
            for p in others:
                copy(top.at[z], top.at[z], r["ar2"].at[k, z], dev(near(p), y, x, c))

        def step3():
            for p in others:
                arrive(top.at[near(p)], r["ar2"].at[k, near(p)])
            out[keep, :] = jnp.sum(top[...], axis=0)
            copy(out.at[keep], out.at[keep], r["ar3"].at[k], partner)

        def step4():
            arrive(out.at[give], r["ar3"].at[k])

        return [step0, step1, step2, step3, step4]

    def spread_sum(k, value):
        here = y * X + x
        q = rank // (C * X * Y)
        src, inc, red, mid, top, res = (r[n].at[k] for n in ("s_src", "s_in", "s_red", "s_mid", "s_top", "s_res"))

        def step0():
            v = value()
            for i in range(C):
                for w in range(X * Y):
                    first = (i * X * Y + w) * q
                    src[i, w] = v[first : first + q]
            copy(src.at[1 - c], inc, r["sp0"].at[k], partner)

        def step1():
            arrive(inc, r["sp0"].at[k])
            red[...] = src[c] + inc[...]
            mid[here] = red[here]
            for i, (dy, dx) in enumerate(plane):
                yy, xx = at(y, dy, Y), at(x, dx, X)
                copy(red.at[yy * X + xx], mid.at[here], r["sp1"].at[k, i], dev(z, yy, xx, c))

        def step2():
            for i, (dy, dx) in enumerate(plane):
                arrive(mid.at[at(y, -dy, Y) * X + at(x, -dx, X)], r["sp1"].at[k, i])
            top[z] = jnp.sum(mid[...], axis=0)
            for p in others:
                copy(top.at[z], top.at[z], r["sp2"].at[k, z], dev(near(p), y, x, c))

        def step3():
            for p in others:
                arrive(top.at[near(p)], r["sp2"].at[k, near(p)])
            res[c, here] = jnp.sum(top[...], axis=0)
            for i, (dy, dx) in enumerate(plane):
                copy(res.at[c, here], res.at[c, here], r["sp3"].at[k, i],
                     dev(z, at(y, dy, Y), at(x, dx, X), c))

        def step4():
            for i, (dy, dx) in enumerate(plane):
                arrive(res.at[c, at(y, -dy, Y) * X + at(x, -dx, X)], r["sp3"].at[k, i])
            copy(res.at[c], res.at[c], r["sp4"].at[k], partner)

        def step5():
            arrive(res.at[1 - c], r["sp4"].at[k])

        def total():
            return jnp.concatenate([res[i, w] for i in range(C) for w in range(X * Y)], axis=0)

        return [step0, step1, step2, step3, step4, step5], total

    aug = r["aug"]
    lane = lax.broadcasted_iota(jnp.int32, (rank, rank), 1)
    row_of = lax.broadcasted_iota(jnp.int32, (rank, rank), 0)

    def eliminate(p, _):
        first = pl.multiple_of(p * PANEL, PANEL)
        lanes = lane[:PANEL]
        index = row_of[:PANEL, :1]
        block = aug[pl.ds(first, PANEL), :]
        left = block[:, :rank]
        cols = [
            jnp.sum(jnp.where(lanes == first + k, left, 0.0), axis=1, keepdims=True)
            for k in range(PANEL)
        ]
        scale = jnp.zeros((PANEL, 1), F32)
        for k in range(PANEL):
            inv = 1.0 / cols[k][k : k + 1]
            f = jnp.where(index > k, cols[k] * inv, 0.0)
            for m in range(k + 1, PANEL):
                cols[m] = cols[m] - f * cols[m][k : k + 1]
            block = block - f * block[k : k + 1]
            scale = jnp.where(index == k, inv, scale)
        u = thirds(jnp.where(lanes >= first + PANEL, block[:, :rank] * scale, 0.0))
        v = thirds(block)
        lhs = jnp.concatenate([u[i] for i in (0, 0, 0, 1, 1, 2)], axis=0).astype(BF16)
        rhs = jnp.concatenate([v[i] for i in (0, 1, 2, 0, 1, 0)], axis=0).astype(BF16)
        aug[...] = aug[...] - dot(lhs, rhs, ((0,), (0,)))
        aug[pl.ds(first, PANEL), :] = block
        return 0

    def begin():
        aug[:, :rank] = gram_total()
        aug[:, rank:] = jnp.where(lane == row_of, 1.0, 0.0)

    def chol(first, last):
        lax.fori_loop(first, last, eliminate, 0)

    def finish():
        diag = jnp.sum(jnp.where(lane == row_of, aug[:, :rank], 0.0), axis=1, keepdims=True)
        inverse = aug[:, rank:] * lax.rsqrt(diag)
        inverse_out[...] = inverse
        basis[...] = jnp.sqrt(F32(total_pixels)) * exact(sketched, inverse, ((1,), (1,)))
        projection[...] = exact(raw, inverse, ((1,), (1,)))

    part, q = r["part"], r["q"]

    def rs1(s):
        zo = near(s)
        g_hi, g_lo = split(green[:, pl.ds(pl.multiple_of(zo * slab, 128), slab)])
        tall = jnp.concatenate([g_hi, g_hi, g_lo, g_lo], axis=0)
        part[s] = dot(tall, packed, ((0,), (0,))).reshape(Y, X, C, rows, rank)
        copy(part.at[s, :, :, 1 - c], r["rd"].at[s], r["rsd"].at[s], partner)

    def rs2(s):
        arrive(r["rd"].at[s], r["rsd"].at[s])
        q[s] = part[s, :, :, c] + r["rd"][s]
        for dy in range(1, Y):
            copy(q.at[s, at(y, dy, Y), :, part_a], r["rya"].at[s, dy], r["rsya"].at[s, dy],
                 dev(z, at(y, dy, Y), x, c))
        for dx in range(1, X):
            copy(q.at[s, :, at(x, dx, X), part_b], r["rxb"].at[s, dx], r["rsxb"].at[s, dx],
                 dev(z, y, at(x, dx, X), c))

    def rs3(s):
        total = q[s, y, :, part_a]
        for dy in range(1, Y):
            arrive(r["rya"].at[s, dy], r["rsya"].at[s, dy])
            total = total + r["rya"][s, dy]
        r["qa"][s] = total
        for dx in range(1, X):
            copy(r["qa"].at[s, at(x, dx, X)], r["rxa"].at[s, dx], r["rsxa"].at[s, dx],
                 dev(z, y, at(x, dx, X), c))
        total = q[s, :, x, part_b]
        for dx in range(1, X):
            arrive(r["rxb"].at[s, dx], r["rsxb"].at[s, dx])
            total = total + r["rxb"][s, dx]
        r["qb"][s] = total
        for dy in range(1, Y):
            copy(r["qb"].at[s, at(y, dy, Y)], r["ryb"].at[s, dy], r["rsyb"].at[s, dy],
                 dev(z, at(y, dy, Y), x, c))

    def rs4(s):
        total = r["qa"][s, x]
        for dx in range(1, X):
            arrive(r["rxa"].at[s, dx], r["rsxa"].at[s, dx])
            total = total + r["rxa"][s, dx]
        r["fin"][s, part_a] = total
        total = r["qb"][s, y]
        for dy in range(1, Y):
            arrive(r["ryb"].at[s, dy], r["rsyb"].at[s, dy])
            total = total + r["ryb"][s, dy]
        r["fin"][s, part_b] = total
        if s:
            copy(r["fin"].at[s], r["rz"].at[z], r["rsz"].at[z], dev(near(s), y, x, c))

    gram, gram_total = spread_sum(0, lambda: exact(sketched, sketched, ((0,), (0,))))
    last = Z + 2
    extra = {0: gram[:1], 1: gram[1:2], last - 3: gram[2:3], last - 1: gram[3:4], last: gram[4:5]}
    pipeline([rs1, rs2, rs3, rs4], range(Z)[::-1], extra)

    raw = r["fin"][0]
    for p in others:
        arrive(r["rz"].at[near(p)], r["rsz"].at[near(p)])
        raw = raw + r["rz"][near(p)]
    spec_sum = all_sum(0, lambda: exact(raw, raw, ((0,), (0,))), spec)
    panels = rank // PANEL
    spec_sum[0]()
    gram[5]()
    begin()
    spec_sum[1]()
    chol(0, panels * 2 // 5)
    spec_sum[2]()
    chol(panels * 2 // 5, panels)
    spec_sum[3]()
    finish()
    spec_sum[4]()
    for d in sends:
        d.wait_send()


def finish_kernel(patches, basis_in, projection_in, inverse_in, spec_in, basis, projection, spectrum):
    inverse = inverse_in[...]
    basis[...] = basis_in[...]
    projection[...] = projection_in[...]
    spectrum[...] = exact(exact(inverse, spec_in[...]), inverse, ((1,), (1,))) / F32(patches)


def body(grid, green, sketch):
    C, X, Y, Z = grid
    rows, rank = sketch.shape
    pixels, patches = green.shape
    half_a = (rows // 2 + 7) // 8 * 8
    half_b = rows - half_a
    plane = X * Y - 1
    few = rank // (C * X * Y)

    def vmem(*shape):
        return pltpu.VMEM(shape, F32)

    def dma(*shape):
        return pltpu.SemaphoreType.DMA(shape)

    per_slab = 2 * (X - 1) + 2 * (Y - 1) + 1
    sends = 2 * (Z * per_slab + Z - 1) + 2 * (2 + 2 * plane + Z - 1)
    scratch = dict(
        gat=vmem(Z, Y, X, C, rows, rank), sketched=vmem(pixels, rank),
        part=vmem(Z, Y, X, C, rows, rank), rd=vmem(Z, Y, X, rows, rank),
        q=vmem(Z, Y, X, rows, rank),
        rya=vmem(Z, Y, X, half_a, rank), rxb=vmem(Z, X, Y, half_b, rank),
        qa=vmem(Z, X, half_a, rank), qb=vmem(Z, Y, half_b, rank),
        rxa=vmem(Z, X, half_a, rank), ryb=vmem(Z, Y, half_b, rank),
        fin=vmem(Z, rows, rank), rz=vmem(Z, rows, rank),
        ar_src=vmem(1, rank, rank), ar_in=vmem(1, rank // C, rank),
        ar_mid=vmem(1, X * Y, rank // C, rank), ar_top=vmem(1, Z, rank // C, rank),
        s_src=vmem(2, C, X * Y, few, rank), s_in=vmem(2, X * Y, few, rank),
        s_red=vmem(2, X * Y, few, rank), s_mid=vmem(2, X * Y, few, rank),
        s_top=vmem(2, Z, few, rank), s_res=vmem(2, C, X * Y, few, rank),
        green=vmem(pixels, patches), sketch=vmem(rows, rank), aug=vmem(rank, 2 * rank),
        send=dma(sends), load=dma(2),
        agz=dma(Z), agxa=dma(Z, X), agyb=dma(Z, Y), agya=dma(Z, Y), agxb=dma(Z, X), agd=dma(Z),
        rsd=dma(Z), rsya=dma(Z, Y), rsxb=dma(Z, X), rsxa=dma(Z, X), rsyb=dma(Z, Y), rsz=dma(Z),
        ar0=dma(1), ar1=dma(1, plane), ar2=dma(1, Z), ar3=dma(1),
        sp0=dma(2), sp1=dma(2, plane), sp2=dma(2, Z), sp3=dma(2, plane), sp4=dma(2),
    )
    total_pixels = pixels * C * X * Y * Z
    tall = jax.ShapeDtypeStruct((pixels, rank), F32)
    wide = jax.ShapeDtypeStruct((rows, rank), F32)
    square = jax.ShapeDtypeStruct((rank, rank), F32)
    whole = pl.BlockSpec(memory_space=pltpu.VMEM)
    parts = pl.pallas_call(
        functools.partial(kernel, grid, total_pixels),
        out_shape=(tall, wide, square, square),
        in_specs=[pl.BlockSpec(memory_space=pl.ANY)] * 2,
        out_specs=(whole,) * 4,
        scratch_shapes=[scratch],
        compiler_params=pltpu.CompilerParams(
            collective_id=0, has_side_effects=True, vmem_limit_bytes=63 * 1024 * 1024
        ),
    )(green, sketch)
    return pl.pallas_call(
        functools.partial(finish_kernel, patches),
        out_shape=(tall, wide, square),
        in_specs=[whole] * 4,
        out_specs=(whole,) * 3,
    )(*parts)


def solution(mesh):
    grid = grid_of(mesh.shape["pix"])
    in_specs = (P("pix", None), P("pix", None))
    out_specs = (P("pix", None), P("pix", None), P())
    return jax.shard_map(
        functools.partial(body, grid), mesh=mesh, in_specs=in_specs, out_specs=out_specs, check_vma=False
    )
```

profile of v0, /device:TPU:0, one launch (start us, length us, event | category | flops | bytes accessed | tf_op | source)
XLA Modules:
  0.0 63.3 jit_solution(9390257459188231001)
XLA Ops:
  0.6 60.6 %shard_map.49 = (f32[64,128]{1,0:T(8,128)}, f32[192,128]{1,0:T(8,128)}, f32[128,128]{1,0:T(8,128)}, f32[128,128]{1,0:T(8,128)}) custom-call(f32[64,6144]{1,0:T(8,128)} %green_in.1, f32[192,128]{1,0:T(8,128)} %sketch_in.1), custom_call_target="tpu_custom_call" | custom-call | tf_op jit(solution)/shard_map/pallas_call | solution.py:437
  61.2 2.1 %shard_map.50 = (f32[64,128]{1,0:T(8,128)}, f32[192,128]{1,0:T(8,128)}, f32[128,128]{1,0:T(8,128)}) custom-call(f32[64,128]{1,0:T(8,128)} %get-tuple-element.7.basis_in, f32[192,128]{1,0:T(8,128)} %get-tuple-element.8.projection_in, f32[128,128]{1,0:T(8,128)} %get-tuple-element.9.inverse_in, f32[128,128]{1,0:T(8,128)} %get-tuple-element.10.spec_in), custom_call_target="tpu_custom_call" | custom-call | tf_op jit(solution)/shard_map/pallas_call | solution.py:447
where the time goes:
time: 63.5 us; the launch traced here: 63.3 us
  Pallas kernels  62.7 us (99%)
  between operations  0.64 us (1%)
    pallas_call x1, Pallas kernels, body(): pl.pallas_call(functools.partial(kernel, grid, total_pixels), out_shape=(...  60.6 us
    pallas_call x1, Pallas kernels, body(): pl.pallas_call(functools.partial(finish_kernel, patches), out_shape=(tall...  2.07 us

commit v1 on v0

v1 whole, which is shorter than its diff:
```python
import functools
import math

import jax
import jax.numpy as jnp
from jax import lax
from jax.experimental import pallas as pl
from jax.experimental.pallas import tpu as pltpu
from jax.sharding import PartitionSpec as P

MESH = pl.DeviceIdType.MESH
F32 = jnp.float32
BF16 = jnp.bfloat16
PANEL = 8
PARTS = 8


def grid_of(devices):
    cores = 2 if devices % 2 == 0 else 1
    chips = devices // cores
    side = 1
    for k in range(1, chips + 1):
        if chips % (k * k) == 0 and k * k * k <= chips:
            side = k
    return cores, side, side, chips // (side * side)


def order_of(planes):
    table = []
    for z in range(planes):
        rest = sorted((k for k in range(planes) if k != z), key=lambda k: (abs(k - z), k))
        if planes % 2 == 0:
            rest.remove(z ^ 1)
            rest.insert(0, z ^ 1)
        table.append([z] + rest)
    return table


def layout_of(rows, rank):
    parts = 2 if rows % 32 == 0 and rank == 128 else 1
    deep = rows // parts
    return parts, deep, (deep // 2 + 7) // 8 * 8


PLANS = {
    (2, 4): [
        ("ownz", 0, 1), ("ownp", 1), ("ownp", 0), ("ownz", 0, 2), ("ownz", 0, 3), ("zin", 0, 1),
        ("diag", 0, 0), ("ownz", 1, 1), ("zin", 0, 2), ("prep", 1), ("ownz", 1, 2), ("prep", 3),
        ("zin", 0, 3), ("diag", 0, 1), ("ownz", 1, 3), ("prep", 0), ("zin", 1, 1), ("diag", 0, 2),
        ("diag", 0, 3), ("zin", 1, 2), ("zin", 1, 3), ("diag", 1, 1), ("diag", 1, 0), ("fin", 0, 1),
        ("prep", 2), ("fin", 0, 2), ("fin", 0, 3), ("fin", 0, 0), ("diag", 1, 2), ("give", 0),
        ("diag", 1, 3), ("take", 0), ("rs1", 0, 0), ("rs1", 0, 2), ("fin", 1, 1), ("fin", 1, 2),
        ("rs1", 0, 1), ("rs1", 0, 3), ("fin", 1, 0), ("fin", 1, 3), ("give", 1), ("rs2", 0, 2),
        ("take", 1), ("sum", 0, 0), ("rs1", 1, 3), ("rs2", 0, 3), ("rs2", 0, 1), ("rs1", 1, 2),
        ("rs3", 0, 2), ("rs2", 1, 3), ("sum", 0, 1), ("rs1", 1, 1), ("rs3", 0, 3), ("rs1", 1, 0),
        ("rs2", 1, 2), ("rs3", 1, 3), ("rs2", 1, 1), ("rs2", 0, 0), ("sum", 0, 2), ("rs2", 1, 0),
        ("rs3", 0, 1), ("rs3", 1, 2), ("rs3", 1, 1), ("sum", 0, 3), ("panel", 0), ("rs3", 0, 0),
        ("rs3", 1, 0), ("collect",), ("sum", 1, 0), ("panel", 1), ("panel", 2), ("panel", 3),
        ("sum", 1, 1), ("panel", 4), ("panel", 5), ("sum", 1, 2), ("panel", 6), ("panel", 7), ("finish",),
        ("sum", 1, 3),
    ],
}


def schedule(parts, planes):
    tuned = PLANS.get((parts, planes))
    if tuned:
        return tuned
    near = range(planes)
    far = near[::-1]
    plan = []
    for h in range(parts):
        plan += [("ownp", h)] + [("ownz", h, p) for p in near[1:]]
    for h in range(parts):
        for p in near:
            plan += [("zin", h, p)] * (p > 0) + [("diag", h, p)]
    plan += [("prep", p) for p in near]
    for h in range(parts):
        plan += [("fin", h, p) for p in near] + [("give", h)]
    plan += [("take", h) for h in range(parts)] + [("sum", 0, 0)]
    for h in range(parts):
        for p in far:
            plan += [("rs1", h, p), ("rs2", h, p), ("rs3", h, p)]
    plan += [("sum", 0, 1), ("sum", 0, 2), ("collect",), ("sum", 1, 0), ("sum", 0, 3)]
    plan += [("sum", 1, 1)] + [("panel", i) for i in range(PARTS)] + [("finish",)]
    return plan + [("sum", 1, 2), ("sum", 1, 3)]

def split(v):
    hi = v.astype(BF16)
    return hi, (v - hi.astype(F32)).astype(BF16)


def thirds(v):
    a = v.astype(BF16).astype(F32)
    b = (v - a).astype(BF16).astype(F32)
    return a, b, v - a - b


def dot(a, b, dims=((1,), (0,))):
    return lax.dot_general(a, b, (dims, ((), ())), preferred_element_type=F32)


def exact(a, b, dims=((1,), (0,))):
    return lax.dot_general(
        a, b, (dims, ((), ())), precision=lax.Precision.HIGHEST, preferred_element_type=F32
    )


def kernel(grid, total_pixels, green_in, sketch_in, basis, projection, inverse_out, spec, scratch):
    C, X, Y, Z = grid
    assert C == 2
    r = scratch
    me = lax.axis_index("pix")
    c = lax.rem(me, C)
    x = lax.rem(me // C, X)
    y = lax.rem(me // (C * X), Y)
    z = me // (C * X * Y)
    green, sketch, gat, part = r["green"], r["sketch"], r["gat"], r["part"]
    rows, rank = sketch.shape
    pixels = green_in.shape[0]
    both = C * pixels
    G, deep, half = layout_of(rows, rank)
    wide = rank // G
    slab = X * Y * C * rows
    table = order_of(Z)
    mine = pl.ds(pl.multiple_of(c * pixels, 8), pixels)
    low, high = pl.ds(0, half), pl.ds(half, deep - half)
    spans = (low, high)

    def dev(zz, yy, xx, cc):
        return (((zz * Y + yy) * X + xx) * C + cc,)

    def at(v, d, n):
        return lax.rem(v + d + n, n)

    def near(p):
        out = table[0][p]
        for k in range(1, Z):
            out = jnp.where(z == k, table[k][p], out)
        return out

    partner = dev(z, y, x, 1 - c)
    dxs, dys = range(1, X), range(1, Y)
    counter = [0]
    sends = []

    sent = [0]

    def copy(src, dst, recv, to):
        pltpu.make_async_remote_copy(
            src_ref=src, dst_ref=dst, send_sem=r["send"].at[0], recv_sem=recv,
            device_id=to, device_id_type=MESH,
        ).start()
        sent[0] += math.prod(src.shape) // rank

    def tally(count):
        ref = r["tally"].at[pl.ds(0, count)]
        return pltpu.make_async_remote_copy(
            src_ref=ref, dst_ref=ref, send_sem=r["send"].at[0], recv_sem=r["send"].at[0],
            device_id=partner, device_id_type=MESH,
        )

    def arrive(recv, count):
        ref = r["tally"].at[pl.ds(0, count)]
        pltpu.make_async_remote_copy(
            src_ref=ref, dst_ref=ref, send_sem=r["send"].at[0], recv_sem=recv,
            device_id=partner, device_id_type=MESH,
        ).wait_recv()

    def finish_sends():
        tally(sent[0]).wait_send()

    load_sketch = pltpu.make_async_copy(sketch_in, sketch, r["load"].at[0])
    load_green = pltpu.make_async_copy(green_in, green.at[mine], r["load"].at[1])
    load_sketch.start()
    load_green.start()
    barrier = pltpu.get_barrier_semaphore()
    peers = [(partner, None)]
    peers += [(dev(z, y, at(x, dx, X), c), None) for dx in dxs]
    peers += [(dev(z, at(y, dy, Y), x, c), None) for dy in dys]
    peers += [(dev(z - 1, y, x, c), z > 0), (dev(z + 1, y, x, c), z < Z - 1)]

    def greet(peer):
        pl.semaphore_signal(barrier, inc=1, device_id=peer, device_id_type=MESH)

    for peer, when in peers:
        if when is None:
            greet(peer)
        else:
            pl.when(when)(functools.partial(greet, peer))
    lanes = lax.broadcasted_iota(jnp.int32, (deep, rank), 1)
    load_sketch.wait()
    if G == 1:
        gat[0, z, y, x] = sketch[...]
    else:
        top, bottom = sketch[:deep], sketch[deep:]
        gat[0, z, y, x] = jnp.where(lanes < wide, top, pltpu.roll(bottom, wide, 1))
        gat[1, z, y, x] = jnp.where(lanes < wide, pltpu.roll(top, wide, 1), bottom)
    known = len(peers) - 2 + jnp.where(z > 0, 1, 0) + jnp.where(z < Z - 1, 1, 0)
    pl.semaphore_wait(barrier, known)

    rest = deep - half

    def along_x(h, s, k):
        ref = gat.at[h, near(s), y, x, spans[k]]
        for dx in dxs:
            copy(ref, ref, r["agr" if k else "agf"].at[h, s], dev(z, y, at(x, dx, X), c))

    def along_y(h, s, k):
        ref = gat.at[h, near(s), y, x, spans[k]]
        for dy in dys:
            copy(ref, ref, r["agf" if k else "agr"].at[h, s], dev(z, at(y, dy, Y), x, c))

    def in_plane(h, s):
        along_x(h, s, 0)
        along_y(h, s, 1)
        along_x(h, s, 1)
        along_y(h, s, 0)

    def tell(sem, to):
        pl.semaphore_signal(sem, inc=1, device_id=to, device_id_type=MESH)

    def learn(j):
        up, down = r["kup"].at[j], r["kdown"].at[j]
        pl.when((z >= 1) & (z + j < Z))(functools.partial(tell, up, dev(z - 1, y, x, c)))
        pl.when((z + 1 < Z) & (z - j >= 0))(functools.partial(tell, down, dev(z + 1, y, x, c)))

    def known_far(j):
        pl.when(z + 1 + j < Z)(lambda: pl.semaphore_wait(r["kup"].at[j], 1))
        pl.when(z - 1 - j >= 0)(lambda: pl.semaphore_wait(r["kdown"].at[j], 1))

    reach = [0]

    def to_plane(h, p):
        far = max(abs(row[p] - row[0]) for row in table)
        while reach[0] < far - 1:
            reach[0] += 1
            learn(reach[0])
            known_far(reach[0])
        ref = gat.at[h, z, y, x]
        copy(ref, ref, r["agz"].at[h, z], dev(near(p), y, x, c))

    def zin(h, s):
        arrive(r["agz"].at[h, near(s)], deep)
        in_plane(h, s)

    def diag(h, s):
        zc = near(s)
        if dxs or dys:
            arrive(r["agf"].at[h, s], len(dxs) * half + len(dys) * rest)
        for dx in dxs:
            for dy in dys:
                ref = gat.at[h, zc, y, at(x, -dx, X), low]
                copy(ref, ref, r["agr"].at[h, s], dev(z, at(y, dy, Y), x, c))
        for dy in dys:
            for dx in dxs:
                ref = gat.at[h, zc, at(y, -dy, Y), x, high]
                copy(ref, ref, r["agr"].at[h, s], dev(z, y, at(x, dx, X), c))

    def swap():
        pltpu.make_async_remote_copy(
            src_ref=green_in, dst_ref=green.at[mine], send_sem=r["swap_send"].at[0], recv_sem=r["swap"].at[0],
            device_id=partner, device_id_type=MESH,
        ).start()

    def swapped():
        other = green.at[pl.ds(pl.multiple_of((1 - c) * pixels, 8), pixels)]
        load_green.wait()
        pltpu.make_async_remote_copy(
            src_ref=green_in, dst_ref=other, send_sem=r["swap_send"].at[0], recv_sem=r["swap"].at[0],
            device_id=partner, device_id_type=MESH,
        ).wait()

    gl, gt, turned = r["gl"], r["gt"], r["turned"]

    def prep(s):
        g = green[:, pl.ds(pl.multiple_of(near(s) * slab, 128), slab)]
        turned[...] = g.T
        for w in range(X * Y):
            block = turned[pl.ds(pl.multiple_of(w * C * rows + c * rows, 8), rows)]
            hi, lo = split(block)
            gt[s, w] = jnp.concatenate(
                [v[g * deep : (g + 1) * deep] for g in range(G) for v in (hi, lo)], axis=1
            )
            halves = [split(block[g * deep : (g + 1) * deep].T) for g in range(G)]
            gl[s, w] = jnp.concatenate([v[0] for v in halves] + [v[1] for v in halves], axis=0)

    started = set()

    def multiply(h, s):
        if dxs or dys:
            arrive(r["agr"].at[h, s], len(dxs) * rest + len(dys) * half + len(dxs) * len(dys) * deep)
        zc = near(s)
        out = None
        for w in range(X * Y):
            b_hi, b_lo = split(gat[h, zc, w // X, w % X])
            tall = dot(gl[s, w], b_hi)
            term = tall[: G * both] + tall[G * both :] + dot(gl[s, w, : G * both], b_lo)
            out = term if out is None else out + term
        if h in started:
            r["acc"][h] += out
        else:
            started.add(h)
            r["acc"][h] = out

    lane_b = lax.broadcasted_iota(jnp.int32, (both, rank), 1)

    def give(h):
        v = r["acc"][h]
        if G == 2:
            v = jnp.where(lane_b < wide, v[:both], v[both:])
        r["mine"][h] = v
        copy(r["mine"].at[h], r["theirs"].at[h], r["swap"].at[1 + h], partner)

    weights = {}

    def take(h):
        arrive(r["swap"].at[1 + h], both)
        v = r["mine"][h] + r["theirs"][h]
        if G == 2:
            v = v + pltpu.roll(v, wide, 1)
        r["folded"][h] = v
        tall = [v] if G == 1 else [jnp.where(lane_b < wide, v, 0.0), jnp.where(lane_b < wide, 0.0, v)]
        pairs = [split(t) for t in tall]
        for i in range(2):
            r["weights"][h, i] = jnp.concatenate([p[i] for p in pairs for _ in range(2)], axis=0)

    def merge():
        if G == 1:
            r["sketched"][...] = r["folded"][0]
        else:
            r["sketched"][...] = jnp.where(lane_b < wide, r["folded"][0], r["folded"][1])

    here = y * X + x
    q = rank // (C * X * Y)
    cores = [(dy, dx, dc) for dy in range(Y) for dx in range(X) for dc in range(C) if (dy, dx, dc) != (0, 0, 0)]

    def total_sum(k, value, per_chip):
        src, inc, top, res = (r[n].at[k] for n in ("t_src", "t_in", "t_top", "t_res"))
        first = [v for v in cores if not (per_chip and v[2])]

        def step0():
            v = value()
            for i in range(C):
                for w in range(X * Y):
                    begin = (i * X * Y + w) * q
                    src[i, w] = v[begin : begin + q]
            for n, (dy, dx, dc) in enumerate(first):
                yy, xx, cc = at(y, dy, Y), at(x, dx, X), lax.rem(c + dc, C)
                copy(src.at[cc, yy * X + xx], inc.at[n], r["sums"].at[k, 0], dev(z, yy, xx, cc))

        def step1():
            total = src[c, here]
            arrive(r["sums"].at[k, 0], len(first) * q)
            for n in range(len(first)):
                total = total + inc[n]
            top[z] = total
            for p in range(1, Z):
                copy(top.at[z], top.at[z], r["sums"].at[k, 1], dev(near(p), y, x, c))

        def step2():
            if Z > 1:
                arrive(r["sums"].at[k, 1], (Z - 1) * q)
            res[c, here] = jnp.sum(top[...], axis=0)
            for n, (dy, dx, dc) in enumerate(cores):
                yy, xx, cc = at(y, dy, Y), at(x, dx, X), lax.rem(c + dc, C)
                copy(res.at[c, here], res.at[c, here], r["sums"].at[k, 2], dev(z, yy, xx, cc))

        def step3():
            arrive(r["sums"].at[k, 2], len(cores) * q)

        def total():
            return jnp.concatenate([res[i, w] for i in range(C) for w in range(X * Y)], axis=0)

        return [step0, step1, step2, step3], total

    def rs1(h, s):
        for w in range(X * Y):
            part[h, s, w // X, w % X] = dot(gt[s, w], r["weights"][h, 0]) + dot(gt[s, w], r["weights"][h, 1])
        for dy in dys:
            for dx in dxs:
                yy, xx = at(y, dy, Y), at(x, dx, X)
                copy(part.at[h, s, yy, xx, low], r["rda"].at[h, s, dy, dx], r["rsf"].at[h, s],
                     dev(z, yy, x, c))
                copy(part.at[h, s, yy, xx, high], r["rdb"].at[h, s, dy, dx], r["rsf"].at[h, s],
                     dev(z, y, xx, c))
        for dy in dys:
            yy = at(y, dy, Y)
            copy(part.at[h, s, yy, x, low], r["rya"].at[h, s, dy], r["rsr"].at[h, s], dev(z, yy, x, c))
        for dx in dxs:
            xx = at(x, dx, X)
            copy(part.at[h, s, y, xx, high], r["rxb"].at[h, s, dx], r["rsr"].at[h, s], dev(z, y, xx, c))

    def rs2(h, s):
        if dxs and dys:
            arrive(r["rsf"].at[h, s], len(dxs) * len(dys) * deep)
        for dx in dxs:
            xx = at(x, dx, X)
            ref = part.at[h, s, y, xx, low]
            total = ref[...]
            for dy in dys:
                total = total + r["rda"][h, s, dy, dx]
            ref[...] = total
            copy(ref, r["rxa"].at[h, s, dx], r["rsr"].at[h, s], dev(z, y, xx, c))
        for dy in dys:
            yy = at(y, dy, Y)
            ref = part.at[h, s, yy, x, high]
            total = ref[...]
            for dx in dxs:
                total = total + r["rdb"][h, s, dy, dx]
            ref[...] = total
            copy(ref, r["ryb"].at[h, s, dy], r["rsr"].at[h, s], dev(z, yy, x, c))

    fin = r["fin"]

    def rs3(h, s):
        if dxs or dys:
            arrive(r["rsr"].at[h, s], (len(dxs) + len(dys)) * deep)
        total = part[h, s, y, x, low]
        for name, ds in (("rya", dys), ("rxa", dxs)):
            for d in ds:
                total = total + r[name][h, s, d]
        fin[h, s, low] = total
        total = part[h, s, y, x, high]
        for name, ds in (("rxb", dxs), ("ryb", dys)):
            for d in ds:
                total = total + r[name][h, s, d]
        fin[h, s, high] = total
        if s:
            copy(fin.at[h, s], r["rz"].at[h, z], r["rsz"].at[h], dev(near(s), y, x, c))

    def collect():
        got = []
        for h in range(G):
            total = fin[h, 0]
            if Z > 1:
                arrive(r["rsz"].at[h], (Z - 1) * deep)
            for p in range(1, Z):
                total = total + r["rz"][h, near(p)]
            got.append(total)
        if G == 1:
            r["raw"][...] = got[0]
        else:
            r["raw"][:deep] = jnp.where(lanes < wide, got[0], pltpu.roll(got[1], wide, 1))
            r["raw"][deep:] = jnp.where(lanes < wide, pltpu.roll(got[0], wide, 1), got[1])

    aug = r["aug"]
    lane = lax.broadcasted_iota(jnp.int32, (rank, rank), 1)
    row_of = lax.broadcasted_iota(jnp.int32, (rank, rank), 0)

    def eliminate(p, _):
        first = pl.multiple_of(p * PANEL, PANEL)
        lanes = lane[:PANEL]
        index = row_of[:PANEL, :1]
        block = aug[pl.ds(first, PANEL), :]
        left = block[:, :rank]
        cols = [
            jnp.sum(jnp.where(lanes == first + k, left, 0.0), axis=1, keepdims=True)
            for k in range(PANEL)
        ]
        scale = jnp.zeros((PANEL, 1), F32)
        for k in range(PANEL):
            inv = 1.0 / cols[k][k : k + 1]
            f = jnp.where(index > k, cols[k] * inv, 0.0)
            for m in range(k + 1, PANEL):
                cols[m] = cols[m] - f * cols[m][k : k + 1]
            block = block - f * block[k : k + 1]
            scale = jnp.where(index == k, inv, scale)
        u = thirds(jnp.where(lanes >= first + PANEL, block[:, :rank] * scale, 0.0))
        v = thirds(block)
        lhs = jnp.concatenate([u[i] for i in (0, 0, 0, 1, 1, 2)], axis=0).astype(BF16)
        rhs = jnp.concatenate([v[i] for i in (0, 1, 2, 0, 1, 0)], axis=0).astype(BF16)
        aug[...] = aug[...] - dot(lhs, rhs, ((0,), (0,)))
        aug[pl.ds(first, PANEL), :] = block
        return 0

    def begin():
        aug[:, :rank] = gram_total()
        aug[:, rank:] = jnp.where(lane == row_of, 1.0, 0.0)

    def chol(first, last):
        lax.fori_loop(first, last, eliminate, 0)

    def finish():
        diag = jnp.sum(jnp.where(lane == row_of, aug[:, :rank], 0.0), axis=1, keepdims=True)
        inverse = aug[:, rank:] * lax.rsqrt(diag)
        inverse_out[...] = inverse
        basis[...] = jnp.sqrt(F32(total_pixels)) * exact(r["sketched"][mine], inverse, ((1,), (1,)))
        projection[...] = exact(r["raw"][...], inverse, ((1,), (1,)))

    def gram_part():
        v = r["sketched"][...]
        return exact(v, v, ((0,), (0,)))

    def raw_part():
        v = r["raw"][...]
        return exact(v, v, ((0,), (0,)))

    gram, gram_total = total_sum(0, gram_part, True)
    spectrum, spectrum_total = total_sum(1, raw_part, False)
    panels = rank // PANEL

    def panel(i):
        if i == 0:
            begin()
        chol(panels * i // PARTS, panels * (i + 1) // PARTS)

    def send_own(h):
        in_plane(h, 0)
        if h == 0:
            swap()

    def give_take(h):
        take(h)
        if h == G - 1:
            merge()

    def prepare(s):
        if not prepared:
            swapped()
        prepared.add(s)
        prep(s)

    prepared = set()
    steps = dict(
        ownp=send_own, ownz=to_plane, prep=prepare, zin=zin, diag=diag, fin=multiply, give=give,
        take=give_take, rs1=rs1, rs2=rs2, rs3=rs3, collect=collect, sum=lambda k, i: (gram, spectrum)[k][i](),
        panel=panel, finish=finish,
    )
    for name, *index in schedule(G, Z):
        steps[name](*index)
    spec[...] = spectrum_total()
    finish_sends()


def finish_kernel(patches, basis_in, projection_in, inverse_in, spec_in, basis, projection, spectrum):
    inverse = inverse_in[...]
    basis[...] = basis_in[...]
    projection[...] = projection_in[...]
    spectrum[...] = exact(exact(inverse, spec_in[...]), inverse, ((1,), (1,))) / F32(patches)


def body(grid, green, sketch):
    C, X, Y, Z = grid
    rows, rank = sketch.shape
    pixels, patches = green.shape
    G, deep, half = layout_of(rows, rank)
    other = deep - half
    both = C * pixels
    plane = C * X * Y - 1
    few = rank // (C * X * Y)

    def vmem(*shape):
        return pltpu.VMEM(shape, F32)

    def packed(*shape):
        return pltpu.VMEM(shape, BF16)

    def dma(*shape):
        return pltpu.SemaphoreType.DMA(shape)

    flags = pltpu.SemaphoreType.REGULAR((Z,))
    links = X - 1 + Y - 1 + (X - 1) * (Y - 1)
    count = 2 * G * deep * (Z * links + Z - 1) + G * both + 2 * (2 * plane + Z) * few
    scratch = dict(
        green=vmem(both, patches), sketch=vmem(rows, rank), gat=vmem(G, Z, Y, X, deep, rank),
        turned=vmem(X * Y * C * rows, both),
        gl=packed(Z, X * Y, 2 * G * both, deep), gt=packed(Z, X * Y, deep, 2 * G * both),
        acc=vmem(G, G * both, rank), mine=vmem(G, both, rank), theirs=vmem(G, both, rank),
        folded=vmem(G, both, rank), weights=packed(G, 2, 2 * G * both, rank), sketched=vmem(both, rank),
        part=vmem(G, Z, Y, X, deep, rank),
        rda=vmem(G, Z, Y, X, half, rank), rdb=vmem(G, Z, Y, X, other, rank),
        rya=vmem(G, Z, Y, half, rank), rxb=vmem(G, Z, X, other, rank),
        rxa=vmem(G, Z, X, half, rank), ryb=vmem(G, Z, Y, other, rank),
        fin=vmem(G, Z, deep, rank), rz=vmem(G, Z, deep, rank), raw=vmem(rows, rank),
        t_src=vmem(2, C, X * Y, few, rank), t_in=vmem(2, plane, few, rank),
        t_top=vmem(2, Z, few, rank), t_res=vmem(2, C, X * Y, few, rank),
        aug=vmem(rank, 2 * rank), kup=flags, kdown=flags,
        tally=vmem(count, rank),
        send=dma(1), load=dma(2), swap=dma(1 + G), swap_send=dma(1),
        agz=dma(G, Z), agf=dma(G, Z), agr=dma(G, Z),
        rsf=dma(G, Z), rsr=dma(G, Z), rsz=dma(G), sums=dma(2, 3),
    )
    total_pixels = pixels * C * X * Y * Z
    tall = jax.ShapeDtypeStruct((pixels, rank), F32)
    wide = jax.ShapeDtypeStruct((rows, rank), F32)
    square = jax.ShapeDtypeStruct((rank, rank), F32)
    whole = pl.BlockSpec(memory_space=pltpu.VMEM)
    parts = pl.pallas_call(
        functools.partial(kernel, grid, total_pixels),
        out_shape=(tall, wide, square, square),
        in_specs=[pl.BlockSpec(memory_space=pl.ANY)] * 2,
        out_specs=(whole,) * 4,
        scratch_shapes=[scratch],
        compiler_params=pltpu.CompilerParams(
            collective_id=0, has_side_effects=True, vmem_limit_bytes=63 * 1024 * 1024
        ),
    )(green, sketch)
    return pl.pallas_call(
        functools.partial(finish_kernel, patches),
        out_shape=(tall, wide, square),
        in_specs=[whole] * 4,
        out_specs=(whole,) * 3,
    )(*parts)


def solution(mesh):
    grid = grid_of(mesh.shape["pix"])
    in_specs = (P("pix", None), P("pix", None))
    out_specs = (P("pix", None), P("pix", None), P())
    return jax.shard_map(
        functools.partial(body, grid), mesh=mesh, in_specs=in_specs, out_specs=out_specs, check_vma=False
    )
```

time: 63.5 us -> 55.5 us (0.87)
  Pallas kernels: 62.7 us -> 54.7 us
    pallas_call x1, Pallas kernels: 60.6 us -> 52.6 us  [body(): pl.pallas_call(functools.partial(kernel, grid, total_pixels), out_shape=(...]
where the time goes in v1:
time: 55.5 us; the launch traced here: 55.4 us
  Pallas kernels  54.7 us (99%)
  between operations  0.64 us (1%)
    pallas_call x1, Pallas kernels, body(): pl.pallas_call(functools.partial(kernel, grid, total_pixels), out_shape=(...  52.6 us
    pallas_call x1, Pallas kernels, body(): pl.pallas_call(functools.partial(finish_kernel, patches), out_shape=(tall...  2.07 us

profile of v1, /device:TPU:0, one launch (start us, length us, event | category | flops | bytes accessed | tf_op | source)
XLA Modules:
  0.0 55.4 jit_solution(9576053632763725832)
XLA Ops:
  0.6 52.6 %shard_map.49 = (f32[64,128]{1,0:T(8,128)}, f32[192,128]{1,0:T(8,128)}, f32[128,128]{1,0:T(8,128)}, f32[128,128]{1,0:T(8,128)}) custom-call(f32[64,6144]{1,0:T(8,128)} %green_in.1, f32[192,128]{1,0:T(8,128)} %sketch_in.1), custom_call_target="tpu_custom_call" | custom-call | tf_op jit(solution)/shard_map/pallas_call | solution.py:589
  53.3 2.1 %shard_map.50 = (f32[64,128]{1,0:T(8,128)}, f32[192,128]{1,0:T(8,128)}, f32[128,128]{1,0:T(8,128)}) custom-call(f32[64,128]{1,0:T(8,128)} %get-tuple-element.7.basis_in, f32[192,128]{1,0:T(8,128)} %get-tuple-element.8.projection_in, f32[128,128]{1,0:T(8,128)} %get-tuple-element.9.inverse_in, f32[128,128]{1,0:T(8,128)} %get-tuple-element.10.spec_in), custom_call_target="tpu_custom_call" | custom-call | tf_op jit(solution)/shard_map/pallas_call | solution.py:599

commit v2 on v1

--- a/solution.py
+++ b/solution.py
@@ -146,17 +146,18 @@
 
     sent = [0]
 
-    def copy(src, dst, recv, to):
+    def copy(src, dst, recv, to, leaves=None):
         pltpu.make_async_remote_copy(
-            src_ref=src, dst_ref=dst, send_sem=r["send"].at[0], recv_sem=recv,
+            src_ref=src, dst_ref=dst, send_sem=r["send"].at[0] if leaves is None else leaves, recv_sem=recv,
             device_id=to, device_id_type=MESH,
         ).start()
-        sent[0] += math.prod(src.shape) // rank
-
-    def tally(count):
+        if leaves is None:
+            sent[0] += math.prod(src.shape) // rank
+
+    def tally(count, leaves):
         ref = r["tally"].at[pl.ds(0, count)]
         return pltpu.make_async_remote_copy(
-            src_ref=ref, dst_ref=ref, send_sem=r["send"].at[0], recv_sem=r["send"].at[0],
+            src_ref=ref, dst_ref=ref, send_sem=leaves, recv_sem=leaves,
             device_id=partner, device_id_type=MESH,
         )
 
@@ -168,7 +169,9 @@
         ).wait_recv()
 
     def finish_sends():
-        tally(sent[0]).wait_send()
+        tally(sent[0], r["send"].at[0]).wait_send()
+        drain_gram()
+        drain_spectrum()
 
     load_sketch = pltpu.make_async_copy(sketch_in, sketch, r["load"].at[0])
     load_green = pltpu.make_async_copy(green_in, green.at[mine], r["load"].at[1])
@@ -331,48 +334,81 @@
         else:
             r["sketched"][...] = jnp.where(lane_b < wide, r["folded"][0], r["folded"][1])
 
+    owner = C - 1
+    owns = c == owner
     here = y * X + x
-    q = rank // (C * X * Y)
-    cores = [(dy, dx, dc) for dy in range(Y) for dx in range(X) for dc in range(C) if (dy, dx, dc) != (0, 0, 0)]
+    q = rank // (X * Y)
+    spots = [(dy, dx) for dy in range(Y) for dx in range(X)]
+    n = len(spots)
 
     def total_sum(k, value, per_chip):
         src, inc, top, res = (r[n].at[k] for n in ("t_src", "t_in", "t_top", "t_res"))
-        first = [v for v in cores if not (per_chip and v[2])]
+        leaves = r["sums_send"].at[k]
+
+        def send(ref, dst, step, to):
+            copy(ref, dst, r["sums"].at[k, step], to, leaves)
+
+        def scatter(skip):
+            for dy, dx in spots[skip:]:
+                yy, xx = at(y, dy, Y), at(x, dx, X)
+                send(src.at[yy * X + xx], inc.at[c, dy * X + dx], 0, dev(z, yy, xx, owner))
 
         def step0():
-            v = value()
-            for i in range(C):
-                for w in range(X * Y):
-                    begin = (i * X * Y + w) * q
-                    src[i, w] = v[begin : begin + q]
-            for n, (dy, dx, dc) in enumerate(first):
-                yy, xx, cc = at(y, dy, Y), at(x, dx, X), lax.rem(c + dc, C)
-                copy(src.at[cc, yy * X + xx], inc.at[n], r["sums"].at[k, 0], dev(z, yy, xx, cc))
+            def fill():
+                v = value()
+                for w in range(n):
+                    src[w] = v[w * q : (w + 1) * q]
+
+            if per_chip:
+                @pl.when(owns)
+                def _():
+                    fill()
+                    scatter(1)
+            else:
+                fill()
+                pl.when(owns)(lambda: scatter(1))
+                pl.when(~owns)(lambda: scatter(0))
 
         def step1():
-            total = src[c, here]
-            arrive(r["sums"].at[k, 0], len(first) * q)
-            for n in range(len(first)):
-                total = total + inc[n]
-            top[z] = total
-            for p in range(1, Z):
-                copy(top.at[z], top.at[z], r["sums"].at[k, 1], dev(near(p), y, x, c))
+            @pl.when(owns)
+            def _():
+                total = src[here]
+                arrive(r["sums"].at[k, 0], (n - 1 if per_chip else 2 * n - 1) * q)
+                for i in range(n):
+                    if i:
+                        total = total + inc[owner, i]
+                    if not per_chip:
+                        total = total + inc[0, i]
+                top[z] = total
+                for p in range(1, Z):
+                    send(top.at[z], top.at[z], 1, dev(near(p), y, x, owner))
 
         def step2():
-            if Z > 1:
-                arrive(r["sums"].at[k, 1], (Z - 1) * q)
-            res[c, here] = jnp.sum(top[...], axis=0)
-            for n, (dy, dx, dc) in enumerate(cores):
-                yy, xx, cc = at(y, dy, Y), at(x, dx, X), lax.rem(c + dc, C)
-                copy(res.at[c, here], res.at[c, here], r["sums"].at[k, 2], dev(z, yy, xx, cc))
+            @pl.when(owns)
+            def _():
+                if Z > 1:
+                    arrive(r["sums"].at[k, 1], (Z - 1) * q)
+                res[here] = jnp.sum(top[...], axis=0)
+                for dy, dx in spots[::-1]:
+                    yy, xx = at(y, dy, Y), at(x, dx, X)
+                    for cc in range(C):
+                        if (dy, dx) != (0, 0) or cc != owner:
+                            send(res.at[here], res.at[here], 2, dev(z, yy, xx, cc))
 
         def step3():
-            arrive(r["sums"].at[k, 2], len(cores) * q)
+            pl.when(~owns)(lambda: arrive(r["sums"].at[k, 2], n * q))
+            if n > 1:
+                pl.when(owns)(lambda: arrive(r["sums"].at[k, 2], (n - 1) * q))
+
+        def drain():
+            pl.when(owns)(lambda: tally((n - 1 + Z - 1 + 2 * n - 1) * q, leaves).wait_send())
+            if not per_chip:
+                pl.when(~owns)(lambda: tally(n * q, leaves).wait_send())
 
         def total():
-            return jnp.concatenate([res[i, w] for i in range(C) for w in range(X * Y)], axis=0)
-
-        return [step0, step1, step2, step3], total
+            return jnp.concatenate([res[w] for w in range(n)], axis=0)
+
+        return [step0, step1, step2, step3], total, drain
 
     def rs1(h, s):
         for w in range(X * Y):
@@ -496,8 +532,8 @@
         v = r["raw"][...]
         return exact(v, v, ((0,), (0,)))
 
-    gram, gram_total = total_sum(0, gram_part, True)
-    spectrum, spectrum_total = total_sum(1, raw_part, False)
+    gram, gram_total, drain_gram = total_sum(0, gram_part, True)
+    spectrum, spectrum_total, drain_spectrum = total_sum(1, raw_part, False)
     panels = rank // PANEL
 
     def panel(i):
@@ -547,8 +583,7 @@
     G, deep, half = layout_of(rows, rank)
     other = deep - half
     both = C * pixels
-    plane = C * X * Y - 1
-    few = rank // (C * X * Y)
+    few = rank // (X * Y)
 
     def vmem(*shape):
         return pltpu.VMEM(shape, F32)
@@ -561,7 +596,7 @@
 
     flags = pltpu.SemaphoreType.REGULAR((Z,))
     links = X - 1 + Y - 1 + (X - 1) * (Y - 1)
-    count = 2 * G * deep * (Z * links + Z - 1) + G * both + 2 * (2 * plane + Z) * few
+    count = 2 * G * deep * (Z * links + Z - 1) + G * both
     scratch = dict(
         green=vmem(both, patches), sketch=vmem(rows, rank), gat=vmem(G, Z, Y, X, deep, rank),
         turned=vmem(X * Y * C * rows, both),
@@ -573,13 +608,13 @@
         rya=vmem(G, Z, Y, half, rank), rxb=vmem(G, Z, X, other, rank),
         rxa=vmem(G, Z, X, half, rank), ryb=vmem(G, Z, Y, other, rank),
         fin=vmem(G, Z, deep, rank), rz=vmem(G, Z, deep, rank), raw=vmem(rows, rank),
-        t_src=vmem(2, C, X * Y, few, rank), t_in=vmem(2, plane, few, rank),
-        t_top=vmem(2, Z, few, rank), t_res=vmem(2, C, X * Y, few, rank),
+        t_src=vmem(2, X * Y, few, rank), t_in=vmem(2, C, X * Y, few, rank),
+        t_top=vmem(2, Z, few, rank), t_res=vmem(2, X * Y, few, rank),
         aug=vmem(rank, 2 * rank), kup=flags, kdown=flags,
         tally=vmem(count, rank),
         send=dma(1), load=dma(2), swap=dma(1 + G), swap_send=dma(1),
         agz=dma(G, Z), agf=dma(G, Z), agr=dma(G, Z),
-        rsf=dma(G, Z), rsr=dma(G, Z), rsz=dma(G), sums=dma(2, 3),
+        rsf=dma(G, Z), rsr=dma(G, Z), rsz=dma(G), sums=dma(2, 3), sums_send=dma(2),
     )
     total_pixels = pixels * C * X * Y * Z
     tall = jax.ShapeDtypeStruct((pixels, rank), F32)

time: 55.5 us -> 54.1 us (0.975)
  Pallas kernels: 54.7 us -> 53.3 us
    pallas_call x1, Pallas kernels: 52.6 us -> 51.2 us  [body(): pl.pallas_call(functools.partial(kernel, grid, total_pixels), out_shape=(...]
where the time goes in v2:
time: 54.1 us; the launch traced here: 53.9 us
  Pallas kernels  53.3 us (99%)
  between operations  0.64 us (1%)
    pallas_call x1, Pallas kernels, body(): pl.pallas_call(functools.partial(kernel, grid, total_pixels), out_shape=(...  51.2 us
    pallas_call x1, Pallas kernels, body(): pl.pallas_call(functools.partial(finish_kernel, patches), out_shape=(tall...  2.07 us

profile of v2, /device:TPU:0, one launch (start us, length us, event | category | flops | bytes accessed | tf_op | source)
XLA Modules:
  0.0 53.9 jit_solution(7446696931468471091)
XLA Ops:
  0.6 51.2 %shard_map.49 = (f32[64,128]{1,0:T(8,128)}, f32[192,128]{1,0:T(8,128)}, f32[128,128]{1,0:T(8,128)}, f32[128,128]{1,0:T(8,128)}) custom-call(f32[64,6144]{1,0:T(8,128)} %green_in.1, f32[192,128]{1,0:T(8,128)} %sketch_in.1), custom_call_target="tpu_custom_call" | custom-call | tf_op jit(solution)/shard_map/pallas_call | solution.py:624
  51.8 2.1 %shard_map.50 = (f32[64,128]{1,0:T(8,128)}, f32[192,128]{1,0:T(8,128)}, f32[128,128]{1,0:T(8,128)}) custom-call(f32[64,128]{1,0:T(8,128)} %get-tuple-element.7.basis_in, f32[192,128]{1,0:T(8,128)} %get-tuple-element.8.projection_in, f32[128,128]{1,0:T(8,128)} %get-tuple-element.9.inverse_in, f32[128,128]{1,0:T(8,128)} %get-tuple-element.10.spec_in), custom_call_target="tpu_custom_call" | custom-call | tf_op jit(solution)/shard_map/pallas_call | solution.py:634

commit v3 on v2

--- a/solution.py
+++ b/solution.py
@@ -13,6 +13,8 @@
 BF16 = jnp.bfloat16
 PANEL = 8
 PARTS = 8
+VLIM = 53.63
+KEEP = 6
 
 
 def grid_of(devices):
@@ -36,28 +38,30 @@
     return table
 
 
-def layout_of(rows, rank):
+def layout_of(grid, rows, rank):
+    C, X, Y, Z = grid
     parts = 2 if rows % 32 == 0 and rank == 128 else 1
     deep = rows // parts
-    return parts, deep, (deep // 2 + 7) // 8 * 8
+    half = (deep // 2 + 7) // 8 * 8
+    keep = min(max(8, KEEP * half // 6 // 8 * 8), deep - half)
+    return parts, deep, half, keep if Z % 2 == 0 and X * Y > 1 and 0 < keep < half else None
 
 
 PLANS = {
     (2, 4): [
-        ("ownz", 0, 1), ("ownp", 1), ("ownp", 0), ("ownz", 0, 2), ("ownz", 0, 3), ("zin", 0, 1),
-        ("diag", 0, 0), ("ownz", 1, 1), ("zin", 0, 2), ("prep", 1), ("ownz", 1, 2), ("prep", 3),
-        ("zin", 0, 3), ("diag", 0, 1), ("ownz", 1, 3), ("prep", 0), ("zin", 1, 1), ("diag", 0, 2),
-        ("diag", 0, 3), ("zin", 1, 2), ("zin", 1, 3), ("diag", 1, 1), ("diag", 1, 0), ("fin", 0, 1),
-        ("prep", 2), ("fin", 0, 2), ("fin", 0, 3), ("fin", 0, 0), ("diag", 1, 2), ("give", 0),
-        ("diag", 1, 3), ("take", 0), ("rs1", 0, 0), ("rs1", 0, 2), ("fin", 1, 1), ("fin", 1, 2),
-        ("rs1", 0, 1), ("rs1", 0, 3), ("fin", 1, 0), ("fin", 1, 3), ("give", 1), ("rs2", 0, 2),
-        ("take", 1), ("sum", 0, 0), ("rs1", 1, 3), ("rs2", 0, 3), ("rs2", 0, 1), ("rs1", 1, 2),
-        ("rs3", 0, 2), ("rs2", 1, 3), ("sum", 0, 1), ("rs1", 1, 1), ("rs3", 0, 3), ("rs1", 1, 0),
-        ("rs2", 1, 2), ("rs3", 1, 3), ("rs2", 1, 1), ("rs2", 0, 0), ("sum", 0, 2), ("rs2", 1, 0),
-        ("rs3", 0, 1), ("rs3", 1, 2), ("rs3", 1, 1), ("sum", 0, 3), ("panel", 0), ("rs3", 0, 0),
-        ("rs3", 1, 0), ("collect",), ("sum", 1, 0), ("panel", 1), ("panel", 2), ("panel", 3),
-        ("sum", 1, 1), ("panel", 4), ("panel", 5), ("sum", 1, 2), ("panel", 6), ("panel", 7), ("finish",),
-        ("sum", 1, 3),
+        ("ownz", 0, 1), ("ownz", 1, 1), ("ownp", 1), ("ownz", 0, 2), ("ownp", 0), ("ownz", 0, 3),
+        ("diag", 1, 0), ("zin", 0, 1), ("prep", 1), ("prep", 0), ("diag", 0, 0), ("zin", 0, 2),
+        ("ownz", 1, 2), ("ownz", 1, 3), ("prep", 2), ("zin", 0, 3), ("diag", 0, 1), ("zin", 1, 1),
+        ("diag", 0, 2), ("fin", 0, 0), ("diag", 0, 3), ("fin", 1, 0), ("zin", 1, 2), ("prep", 3),
+        ("zin", 1, 3), ("fin", 0, 1), ("fin", 0, 2), ("diag", 1, 1), ("fin", 0, 3), ("give", 0),
+        ("diag", 1, 2), ("take", 0), ("diag", 1, 3), ("rs1", 0, 3), ("rs1", 0, 2), ("fin", 1, 1),
+        ("rs1", 0, 1), ("fin", 1, 2), ("rs1", 0, 0), ("fin", 1, 3), ("rs2", 0, 3), ("give", 1),
+        ("rs2", 0, 2), ("take", 1), ("rs1", 1, 3), ("sum", 0, 0), ("rs1", 1, 2), ("rs2", 0, 1),
+        ("rs3", 0, 3), ("rs3", 0, 2), ("rs2", 1, 3), ("rs1", 1, 1), ("rs2", 1, 2), ("sum", 0, 1),
+        ("rs1", 1, 0), ("rs3", 0, 1), ("rs3", 1, 3), ("rs2", 1, 1), ("rs2", 0, 0), ("rs3", 1, 2),
+        ("sum", 0, 2), ("rs2", 1, 0), ("rs3", 1, 1), ("rs3", 0, 0), ("sum", 0, 3), ("rs3", 1, 0),
+        ("collect",), ("sum", 1, 0), ("panel", 0), ("panel", 1), ("panel", 2), ("sum", 1, 1), ("panel", 3),
+        ("panel", 4), ("sum", 1, 2), ("panel", 5), ("panel", 6), ("panel", 7), ("finish",), ("sum", 1, 3),
     ],
 }
 
@@ -74,7 +78,7 @@
     for h in range(parts):
         for p in near:
             plan += [("zin", h, p)] * (p > 0) + [("diag", h, p)]
-    plan += [("prep", p) for p in near]
+    plan += [("prep", p) for p in near] + [("share", h) for h in range(parts)]
     for h in range(parts):
         plan += [("fin", h, p) for p in near] + [("give", h)]
     plan += [("take", h) for h in range(parts)] + [("sum", 0, 0)]
@@ -119,13 +123,27 @@
     rows, rank = sketch.shape
     pixels = green_in.shape[0]
     both = C * pixels
-    G, deep, half = layout_of(rows, rank)
+    G, deep, half, keep = layout_of(grid, rows, rank)
     wide = rank // G
     slab = X * Y * C * rows
     table = order_of(Z)
     mine = pl.ds(pl.multiple_of(c * pixels, 8), pixels)
-    low, high = pl.ds(0, half), pl.ds(half, deep - half)
-    spans = (low, high)
+    rest = deep - half
+    other_rows = [(dy, dx) for dy in range(Y) for dx in range(X) if (dy, dx) != (0, 0)]
+    middle = pl.ds(keep or 0, deep - 2 * (keep or 0))
+
+    def low(s):
+        return pl.ds(0, half if keep is None or s != 1 else keep)
+
+    def high(s):
+        return pl.ds(half, rest) if keep is None or s != 1 else pl.ds(deep - keep, keep)
+
+    def n_low(s):
+        return low(s).size
+
+    def n_high(s):
+        return high(s).size
+
 
     def dev(zz, yy, xx, cc):
         return (((zz * Y + yy) * X + xx) * C + cc,)
@@ -202,15 +220,13 @@
     known = len(peers) - 2 + jnp.where(z > 0, 1, 0) + jnp.where(z < Z - 1, 1, 0)
     pl.semaphore_wait(barrier, known)
 
-    rest = deep - half
-
     def along_x(h, s, k):
-        ref = gat.at[h, near(s), y, x, spans[k]]
+        ref = gat.at[h, near(s), y, x, (low, high)[k](s)]
         for dx in dxs:
             copy(ref, ref, r["agr" if k else "agf"].at[h, s], dev(z, y, at(x, dx, X), c))
 
     def along_y(h, s, k):
-        ref = gat.at[h, near(s), y, x, spans[k]]
+        ref = gat.at[h, near(s), y, x, (low, high)[k](s)]
         for dy in dys:
             copy(ref, ref, r["agf" if k else "agr"].at[h, s], dev(z, at(y, dy, Y), x, c))
 
@@ -250,14 +266,14 @@
     def diag(h, s):
         zc = near(s)
         if dxs or dys:
-            arrive(r["agf"].at[h, s], len(dxs) * half + len(dys) * rest)
+            arrive(r["agf"].at[h, s], len(dxs) * n_low(s) + len(dys) * n_high(s))
         for dx in dxs:
             for dy in dys:
-                ref = gat.at[h, zc, y, at(x, -dx, X), low]
+                ref = gat.at[h, zc, y, at(x, -dx, X), low(s)]
                 copy(ref, ref, r["agr"].at[h, s], dev(z, at(y, dy, Y), x, c))
         for dy in dys:
             for dx in dxs:
-                ref = gat.at[h, zc, at(y, -dy, Y), x, high]
+                ref = gat.at[h, zc, at(y, -dy, Y), x, high(s)]
                 copy(ref, ref, r["agr"].at[h, s], dev(z, y, at(x, dx, X), c))
 
     def swap():
@@ -290,9 +306,26 @@
 
     started = set()
 
+    gathered = set()
+
+    def in_hand(h, s):
+        if (dxs or dys) and (h, s) not in gathered:
+            gathered.add((h, s))
+            diags = len(dxs) * len(dys)
+            count = (len(dxs) + diags) * n_high(s) + (len(dys) + diags) * n_low(s)
+            arrive(r["agr"].at[h, s], count)
+
+    def share(h):
+        if keep is not None:
+            in_hand(h, 0)
+            for dy, dx in other_rows:
+                ref = gat.at[h, z, at(y, dy, Y), at(x, dx, X), middle]
+                copy(ref, ref, r["age"].at[h], dev(near(1), y, x, c))
+
     def multiply(h, s):
-        if dxs or dys:
-            arrive(r["agr"].at[h, s], len(dxs) * rest + len(dys) * half + len(dxs) * len(dys) * deep)
+        in_hand(h, s)
+        if s == 1 and keep is not None:
+            arrive(r["age"].at[h], len(other_rows) * middle.size)
         zc = near(s)
         out = None
         for w in range(X * Y):
@@ -410,58 +443,72 @@
 
         return [step0, step1, step2, step3], total, drain
 
+    def head(name, count, *index):
+        return r[name].at[(*index, pl.ds(0, count))]
+
     def rs1(h, s):
         for w in range(X * Y):
             part[h, s, w // X, w % X] = dot(gt[s, w], r["weights"][h, 0]) + dot(gt[s, w], r["weights"][h, 1])
+        if s == 1 and keep is not None:
+            for dy, dx in other_rows:
+                copy(part.at[h, s, at(y, dy, Y), at(x, dx, X), middle], r["ebuf"].at[h, dy, dx],
+                     r["rse"].at[h], dev(near(1), y, x, c))
+        if s == 0 and keep is not None:
+            arrive(r["rse"].at[h], len(other_rows) * middle.size)
+            for dy, dx in other_rows:
+                ref = part.at[h, s, at(y, dy, Y), at(x, dx, X), middle]
+                ref[...] = ref[...] + r["ebuf"][h, dy, dx]
         for dy in dys:
             for dx in dxs:
                 yy, xx = at(y, dy, Y), at(x, dx, X)
-                copy(part.at[h, s, yy, xx, low], r["rda"].at[h, s, dy, dx], r["rsf"].at[h, s],
+                copy(part.at[h, s, yy, xx, low(s)], head("rda", n_low(s), h, s, dy, dx), r["rsf"].at[h, s],
                      dev(z, yy, x, c))
-                copy(part.at[h, s, yy, xx, high], r["rdb"].at[h, s, dy, dx], r["rsf"].at[h, s],
+                copy(part.at[h, s, yy, xx, high(s)], head("rdb", n_high(s), h, s, dy, dx), r["rsf"].at[h, s],
                      dev(z, y, xx, c))
         for dy in dys:
             yy = at(y, dy, Y)
-            copy(part.at[h, s, yy, x, low], r["rya"].at[h, s, dy], r["rsr"].at[h, s], dev(z, yy, x, c))
+            copy(part.at[h, s, yy, x, low(s)], head("rya", n_low(s), h, s, dy), r["rsr"].at[h, s], dev(z, yy, x, c))
         for dx in dxs:
             xx = at(x, dx, X)
-            copy(part.at[h, s, y, xx, high], r["rxb"].at[h, s, dx], r["rsr"].at[h, s], dev(z, y, xx, c))
+            copy(part.at[h, s, y, xx, high(s)], head("rxb", n_high(s), h, s, dx), r["rsr"].at[h, s], dev(z, y, xx, c))
 
     def rs2(h, s):
         if dxs and dys:
-            arrive(r["rsf"].at[h, s], len(dxs) * len(dys) * deep)
+            arrive(r["rsf"].at[h, s], len(dxs) * len(dys) * (n_low(s) + n_high(s)))
         for dx in dxs:
             xx = at(x, dx, X)
-            ref = part.at[h, s, y, xx, low]
+            ref = part.at[h, s, y, xx, low(s)]
             total = ref[...]
             for dy in dys:
-                total = total + r["rda"][h, s, dy, dx]
+                total = total + head("rda", n_low(s), h, s, dy, dx)[...]
             ref[...] = total
-            copy(ref, r["rxa"].at[h, s, dx], r["rsr"].at[h, s], dev(z, y, xx, c))
+            copy(ref, head("rxa", n_low(s), h, s, dx), r["rsr"].at[h, s], dev(z, y, xx, c))
         for dy in dys:
             yy = at(y, dy, Y)
-            ref = part.at[h, s, yy, x, high]
+            ref = part.at[h, s, yy, x, high(s)]
             total = ref[...]
             for dx in dxs:
-                total = total + r["rdb"][h, s, dy, dx]
+                total = total + head("rdb", n_high(s), h, s, dy, dx)[...]
             ref[...] = total
-            copy(ref, r["ryb"].at[h, s, dy], r["rsr"].at[h, s], dev(z, yy, x, c))
+            copy(ref, head("ryb", n_high(s), h, s, dy), r["rsr"].at[h, s], dev(z, yy, x, c))
 
     fin = r["fin"]
 
     def rs3(h, s):
         if dxs or dys:
-            arrive(r["rsr"].at[h, s], (len(dxs) + len(dys)) * deep)
-        total = part[h, s, y, x, low]
+            arrive(r["rsr"].at[h, s], (len(dxs) + len(dys)) * (n_low(s) + n_high(s)))
+        total = part[h, s, y, x, low(s)]
         for name, ds in (("rya", dys), ("rxa", dxs)):
             for d in ds:
-                total = total + r[name][h, s, d]
-        fin[h, s, low] = total
-        total = part[h, s, y, x, high]
+                total = total + head(name, n_low(s), h, s, d)[...]
+        fin[h, s, low(s)] = total
+        total = part[h, s, y, x, high(s)]
         for name, ds in (("rxb", dxs), ("ryb", dys)):
             for d in ds:
-                total = total + r[name][h, s, d]
-        fin[h, s, high] = total
+                total = total + head(name, n_high(s), h, s, d)[...]
+        fin[h, s, high(s)] = total
+        if s == 1 and keep is not None:
+            fin[h, s, middle] = part[h, s, y, x, middle]
         if s:
             copy(fin.at[h, s], r["rz"].at[h, z], r["rsz"].at[h], dev(near(s), y, x, c))
 
@@ -559,7 +606,7 @@
 
     prepared = set()
     steps = dict(
-        ownp=send_own, ownz=to_plane, prep=prepare, zin=zin, diag=diag, fin=multiply, give=give,
+        ownp=send_own, ownz=to_plane, prep=prepare, zin=zin, diag=diag, share=share, fin=multiply, give=give,
         take=give_take, rs1=rs1, rs2=rs2, rs3=rs3, collect=collect, sum=lambda k, i: (gram, spectrum)[k][i](),
         panel=panel, finish=finish,
     )
@@ -580,7 +627,7 @@
     C, X, Y, Z = grid
     rows, rank = sketch.shape
     pixels, patches = green.shape
-    G, deep, half = layout_of(rows, rank)
+    G, deep, half, keep = layout_of(grid, rows, rank)
     other = deep - half
     both = C * pixels
     few = rank // (X * Y)
@@ -596,7 +643,7 @@
 
     flags = pltpu.SemaphoreType.REGULAR((Z,))
     links = X - 1 + Y - 1 + (X - 1) * (Y - 1)
-    count = 2 * G * deep * (Z * links + Z - 1) + G * both
+    count = 2 * G * deep * ((Z + 1) * links + Z - 1) + G * both
     scratch = dict(
         green=vmem(both, patches), sketch=vmem(rows, rank), gat=vmem(G, Z, Y, X, deep, rank),
         turned=vmem(X * Y * C * rows, both),
@@ -607,6 +654,7 @@
         rda=vmem(G, Z, Y, X, half, rank), rdb=vmem(G, Z, Y, X, other, rank),
         rya=vmem(G, Z, Y, half, rank), rxb=vmem(G, Z, X, other, rank),
         rxa=vmem(G, Z, X, half, rank), ryb=vmem(G, Z, Y, other, rank),
+        ebuf=vmem(G, Y, X, max(8, deep - 2 * (keep or 0)), rank),
         fin=vmem(G, Z, deep, rank), rz=vmem(G, Z, deep, rank), raw=vmem(rows, rank),
         t_src=vmem(2, X * Y, few, rank), t_in=vmem(2, C, X * Y, few, rank),
         t_top=vmem(2, Z, few, rank), t_res=vmem(2, X * Y, few, rank),
@@ -614,7 +662,7 @@
         tally=vmem(count, rank),
         send=dma(1), load=dma(2), swap=dma(1 + G), swap_send=dma(1),
         agz=dma(G, Z), agf=dma(G, Z), agr=dma(G, Z),
-        rsf=dma(G, Z), rsr=dma(G, Z), rsz=dma(G), sums=dma(2, 3), sums_send=dma(2),
+        rsf=dma(G, Z), rsr=dma(G, Z), rsz=dma(G), age=dma(G), rse=dma(G), sums=dma(2, 3), sums_send=dma(2),
     )
     total_pixels = pixels * C * X * Y * Z
     tall = jax.ShapeDtypeStruct((pixels, rank), F32)
@@ -628,7 +676,7 @@
         out_specs=(whole,) * 4,
         scratch_shapes=[scratch],
         compiler_params=pltpu.CompilerParams(
-            collective_id=0, has_side_effects=True, vmem_limit_bytes=63 * 1024 * 1024
+            collective_id=0, has_side_effects=True, vmem_limit_bytes=int(VLIM * 2**20)
         ),
     )(green, sketch)
     return pl.pallas_call(
@@ -636,6 +684,7 @@
         out_shape=(tall, wide, square),
         in_specs=[whole] * 4,
         out_specs=(whole,) * 3,
+        compiler_params=pltpu.CompilerParams(vmem_limit_bytes=2**20),
     )(*parts)
 
 

time: 54.1 us -> 50.3 us (0.930)
  Pallas kernels: 53.3 us -> 49.5 us
    pallas_call x1, Pallas kernels: 51.2 us -> 48.4 us  [body(): pl.pallas_call(functools.partial(kernel, grid, total_pixels), out_shape=(...]
    pallas_call x1, Pallas kernels: 2.07 us -> 1.13 us  [body(): pl.pallas_call(functools.partial(finish_kernel, patches), out_shape=(tall...]
where the time goes in v3:
time: 50.3 us; the launch traced here: 50.2 us
  Pallas kernels  49.5 us (98%)
  between operations  0.64 us (1%)
    pallas_call x1, Pallas kernels, body(): pl.pallas_call(functools.partial(kernel, grid, total_pixels), out_shape=(...  48.4 us
    pallas_call x1, Pallas kernels, body(): pl.pallas_call(functools.partial(finish_kernel, patches), out_shape=(tall...  1.13 us

profile of v3, /device:TPU:0, one launch (start us, length us, event | category | flops | bytes accessed | tf_op | source)
XLA Modules:
  0.0 50.2 jit_solution(1001642814454130156)
XLA Ops:
  0.6 48.4 %shard_map.49 = (f32[64,128]{1,0:T(8,128)S(1)}, f32[192,128]{1,0:T(8,128)S(1)}, f32[128,128]{1,0:T(8,128)S(1)}, f32[128,128]{1,0:T(8,128)S(1)}) custom-call(f32[64,6144]{1,0:T(8,128)} %green_in.1, f32[192,128]{1,0:T(8,128)} %sketch_in.1), custom_call_target="tpu_custom_call" | custom-call | tf_op jit(solution)/shard_map/pallas_call | solution.py:672
  49.0 1.1 %shard_map.50 = (f32[64,128]{1,0:T(8,128)}, f32[192,128]{1,0:T(8,128)}, f32[128,128]{1,0:T(8,128)}) custom-call(f32[64,128]{1,0:T(8,128)S(1)} %get-tuple-element.7.basis_in, f32[192,128]{1,0:T(8,128)S(1)} %get-tuple-element.8.projection_in, f32[128,128]{1,0:T(8,128)S(1)} %get-tuple-element.9.inverse_in, f32[128,128]{1,0:T(8,128)S(1)} %get-tuple-element.10.spec_in), custom_call_target="tpu_custom_call" | custom-call | tf_op jit(solution)/shard_map/pallas_call | solution.py:682

commit v4 on v3

--- a/solution.py
+++ b/solution.py
@@ -13,8 +13,10 @@
 BF16 = jnp.bfloat16
 PANEL = 8
 PARTS = 8
+PAIRED = True
 VLIM = 53.63
 KEEP = 6
+SHARES = (0, 0)
 
 
 def grid_of(devices):
@@ -30,8 +32,8 @@
 def order_of(planes):
     table = []
     for z in range(planes):
-        rest = sorted((k for k in range(planes) if k != z), key=lambda k: (abs(k - z), k))
-        if planes % 2 == 0:
+        rest = sorted((k for k in range(planes) if k != z), key=lambda k: (abs(k - z), abs(2 * k - planes + 1)))
+        if planes % 2 == 0 and PAIRED:
             rest.remove(z ^ 1)
             rest.insert(0, z ^ 1)
         table.append([z] + rest)
@@ -49,19 +51,22 @@
 
 PLANS = {
     (2, 4): [
-        ("ownz", 0, 1), ("ownz", 1, 1), ("ownp", 1), ("ownz", 0, 2), ("ownp", 0), ("ownz", 0, 3),
-        ("diag", 1, 0), ("zin", 0, 1), ("prep", 1), ("prep", 0), ("diag", 0, 0), ("zin", 0, 2),
-        ("ownz", 1, 2), ("ownz", 1, 3), ("prep", 2), ("zin", 0, 3), ("diag", 0, 1), ("zin", 1, 1),
-        ("diag", 0, 2), ("fin", 0, 0), ("diag", 0, 3), ("fin", 1, 0), ("zin", 1, 2), ("prep", 3),
-        ("zin", 1, 3), ("fin", 0, 1), ("fin", 0, 2), ("diag", 1, 1), ("fin", 0, 3), ("give", 0),
-        ("diag", 1, 2), ("take", 0), ("diag", 1, 3), ("rs1", 0, 3), ("rs1", 0, 2), ("fin", 1, 1),
-        ("rs1", 0, 1), ("fin", 1, 2), ("rs1", 0, 0), ("fin", 1, 3), ("rs2", 0, 3), ("give", 1),
-        ("rs2", 0, 2), ("take", 1), ("rs1", 1, 3), ("sum", 0, 0), ("rs1", 1, 2), ("rs2", 0, 1),
-        ("rs3", 0, 3), ("rs3", 0, 2), ("rs2", 1, 3), ("rs1", 1, 1), ("rs2", 1, 2), ("sum", 0, 1),
-        ("rs1", 1, 0), ("rs3", 0, 1), ("rs3", 1, 3), ("rs2", 1, 1), ("rs2", 0, 0), ("rs3", 1, 2),
-        ("sum", 0, 2), ("rs2", 1, 0), ("rs3", 1, 1), ("rs3", 0, 0), ("sum", 0, 3), ("rs3", 1, 0),
-        ("collect",), ("sum", 1, 0), ("panel", 0), ("panel", 1), ("panel", 2), ("sum", 1, 1), ("panel", 3),
-        ("panel", 4), ("sum", 1, 2), ("panel", 5), ("panel", 6), ("panel", 7), ("finish",), ("sum", 1, 3),
+        ("ownp", 0), ("ownz", 0, 1), ("ownp", 1), ("ownz", 0, 3), ("ownq", 1), ("ownq", 0), ("ownz", 0, 2),
+        ("diag", 0, 0), ("zin", 0, 1), ("zot", 0, 1), ("prep", 3), ("ownz", 1, 1), ("diag", 1, 0),
+        ("ownz", 1, 3), ("zin", 0, 2), ("ownz", 1, 2), ("zin", 0, 3), ("zot", 0, 2), ("zot", 0, 3),
+        ("prep", 1), ("diag", 0, 1), ("zin", 1, 1), ("prep", 2), ("diag", 0, 2), ("prep", 0),
+        ("diag", 0, 3), ("zin", 1, 2), ("zin", 1, 3), ("zot", 1, 1), ("zot", 1, 2), ("zot", 1, 3),
+        ("fin", 0, 1), ("fin", 0, 0), ("diag", 1, 1), ("fin", 0, 2), ("fin", 0, 3), ("give", 0),
+        ("diag", 1, 2), ("diag", 1, 3), ("take", 0), ("rs1", 0, 1), ("rs1", 0, 2), ("rst", 0, 2),
+        ("rs1", 0, 3), ("fin", 1, 1), ("rst", 0, 1), ("fin", 1, 0), ("fin", 1, 2), ("rst", 0, 3),
+        ("fin", 1, 3), ("give", 1), ("rs2", 0, 1), ("rs2", 0, 2), ("take", 1), ("rs1", 1, 3),
+        ("sum", 0, 0), ("rs1", 1, 1), ("rs2", 0, 3), ("rs1", 1, 2), ("rs3", 0, 1), ("rs3", 0, 2),
+        ("rst", 1, 3), ("rs2", 1, 3), ("rs1", 1, 0), ("sum", 0, 1), ("rst", 1, 2), ("rs2", 1, 1),
+        ("rst", 1, 1), ("rs2", 1, 2), ("rs3", 0, 3), ("rs1", 0, 0), ("rst", 0, 0), ("rst", 1, 0),
+        ("rs3", 1, 3), ("sum", 0, 2), ("rs3", 1, 1), ("rs2", 1, 0), ("rs3", 1, 2), ("rs2", 0, 0),
+        ("sum", 0, 3), ("panel", 0), ("rs3", 1, 0), ("rs3", 0, 0), ("collect",), ("sum", 1, 0),
+        ("panel", 1), ("panel", 2), ("panel", 3), ("sum", 1, 1), ("panel", 4), ("panel", 5), ("sum", 1, 2),
+        ("panel", 6), ("panel", 7), ("finish",), ("sum", 1, 3),
     ],
 }
 
@@ -74,17 +79,17 @@
     far = near[::-1]
     plan = []
     for h in range(parts):
-        plan += [("ownp", h)] + [("ownz", h, p) for p in near[1:]]
+        plan += [("ownp", h), ("ownq", h)] + [("ownz", h, p) for p in near[1:]]
     for h in range(parts):
         for p in near:
-            plan += [("zin", h, p)] * (p > 0) + [("diag", h, p)]
+            plan += [("zin", h, p), ("zot", h, p)] * (p > 0) + [("diag", h, p)]
     plan += [("prep", p) for p in near] + [("share", h) for h in range(parts)]
     for h in range(parts):
         plan += [("fin", h, p) for p in near] + [("give", h)]
     plan += [("take", h) for h in range(parts)] + [("sum", 0, 0)]
     for h in range(parts):
         for p in far:
-            plan += [("rs1", h, p), ("rs2", h, p), ("rs3", h, p)]
+            plan += [("rs1", h, p), ("rst", h, p), ("rs2", h, p), ("rs3", h, p)]
     plan += [("sum", 0, 1), ("sum", 0, 2), ("collect",), ("sum", 1, 0), ("sum", 0, 3)]
     plan += [("sum", 1, 1)] + [("panel", i) for i in range(PARTS)] + [("finish",)]
     return plan + [("sum", 1, 2), ("sum", 1, 3)]
@@ -132,17 +137,19 @@
     other_rows = [(dy, dx) for dy in range(Y) for dx in range(X) if (dy, dx) != (0, 0)]
     middle = pl.ds(keep or 0, deep - 2 * (keep or 0))
 
-    def low(s):
+    keep_g, keep_s = (keep if on else None for on in SHARES)
+
+    def low(s, keep):
         return pl.ds(0, half if keep is None or s != 1 else keep)
 
-    def high(s):
+    def high(s, keep):
         return pl.ds(half, rest) if keep is None or s != 1 else pl.ds(deep - keep, keep)
 
-    def n_low(s):
-        return low(s).size
-
-    def n_high(s):
-        return high(s).size
+    def n_low(s, keep):
+        return low(s, keep).size
+
+    def n_high(s, keep):
+        return high(s, keep).size
 
 
     def dev(zz, yy, xx, cc):
@@ -221,18 +228,20 @@
     pl.semaphore_wait(barrier, known)
 
     def along_x(h, s, k):
-        ref = gat.at[h, near(s), y, x, (low, high)[k](s)]
+        ref = gat.at[h, near(s), y, x, (low, high)[k](s, keep_g)]
         for dx in dxs:
             copy(ref, ref, r["agr" if k else "agf"].at[h, s], dev(z, y, at(x, dx, X), c))
 
     def along_y(h, s, k):
-        ref = gat.at[h, near(s), y, x, (low, high)[k](s)]
+        ref = gat.at[h, near(s), y, x, (low, high)[k](s, keep_g)]
         for dy in dys:
             copy(ref, ref, r["agf" if k else "agr"].at[h, s], dev(z, at(y, dy, Y), x, c))
 
     def in_plane(h, s):
         along_x(h, s, 0)
         along_y(h, s, 1)
+
+    def in_plane_rest(h, s=0):
         along_x(h, s, 1)
         along_y(h, s, 0)
 
@@ -266,14 +275,14 @@
     def diag(h, s):
         zc = near(s)
         if dxs or dys:
-            arrive(r["agf"].at[h, s], len(dxs) * n_low(s) + len(dys) * n_high(s))
+            arrive(r["agf"].at[h, s], len(dxs) * n_low(s, keep_g) + len(dys) * n_high(s, keep_g))
         for dx in dxs:
             for dy in dys:
-                ref = gat.at[h, zc, y, at(x, -dx, X), low(s)]
+                ref = gat.at[h, zc, y, at(x, -dx, X), low(s, keep_g)]
                 copy(ref, ref, r["agr"].at[h, s], dev(z, at(y, dy, Y), x, c))
         for dy in dys:
             for dx in dxs:
-                ref = gat.at[h, zc, at(y, -dy, Y), x, high(s)]
+                ref = gat.at[h, zc, at(y, -dy, Y), x, high(s, keep_g)]
                 copy(ref, ref, r["agr"].at[h, s], dev(z, y, at(x, dx, X), c))
 
     def swap():
@@ -312,11 +321,11 @@
         if (dxs or dys) and (h, s) not in gathered:
             gathered.add((h, s))
             diags = len(dxs) * len(dys)
-            count = (len(dxs) + diags) * n_high(s) + (len(dys) + diags) * n_low(s)
+            count = (len(dxs) + diags) * n_high(s, keep_g) + (len(dys) + diags) * n_low(s, keep_g)
             arrive(r["agr"].at[h, s], count)
 
     def share(h):
-        if keep is not None:
+        if keep_g is not None:
             in_hand(h, 0)
             for dy, dx in other_rows:
                 ref = gat.at[h, z, at(y, dy, Y), at(x, dx, X), middle]
@@ -324,7 +333,7 @@
 
     def multiply(h, s):
         in_hand(h, s)
-        if s == 1 and keep is not None:
+        if s == 1 and keep_g is not None:
             arrive(r["age"].at[h], len(other_rows) * middle.size)
         zc = near(s)
         out = None
@@ -449,11 +458,11 @@
     def rs1(h, s):
         for w in range(X * Y):
             part[h, s, w // X, w % X] = dot(gt[s, w], r["weights"][h, 0]) + dot(gt[s, w], r["weights"][h, 1])
-        if s == 1 and keep is not None:
+        if s == 1 and keep_s is not None:
             for dy, dx in other_rows:
                 copy(part.at[h, s, at(y, dy, Y), at(x, dx, X), middle], r["ebuf"].at[h, dy, dx],
                      r["rse"].at[h], dev(near(1), y, x, c))
-        if s == 0 and keep is not None:
+        if s == 0 and keep_s is not None:
             arrive(r["rse"].at[h], len(other_rows) * middle.size)
             for dy, dx in other_rows:
                 ref = part.at[h, s, at(y, dy, Y), at(x, dx, X), middle]
@@ -461,53 +470,55 @@
         for dy in dys:
             for dx in dxs:
                 yy, xx = at(y, dy, Y), at(x, dx, X)
-                copy(part.at[h, s, yy, xx, low(s)], head("rda", n_low(s), h, s, dy, dx), r["rsf"].at[h, s],
+                copy(part.at[h, s, yy, xx, low(s, keep_s)], head("rda", n_low(s, keep_s), h, s, dy, dx), r["rsf"].at[h, s],
                      dev(z, yy, x, c))
-                copy(part.at[h, s, yy, xx, high(s)], head("rdb", n_high(s), h, s, dy, dx), r["rsf"].at[h, s],
+                copy(part.at[h, s, yy, xx, high(s, keep_s)], head("rdb", n_high(s, keep_s), h, s, dy, dx), r["rsf"].at[h, s],
                      dev(z, y, xx, c))
+
+    def rs_rest(h, s):
         for dy in dys:
             yy = at(y, dy, Y)
-            copy(part.at[h, s, yy, x, low(s)], head("rya", n_low(s), h, s, dy), r["rsr"].at[h, s], dev(z, yy, x, c))
+            copy(part.at[h, s, yy, x, low(s, keep_s)], head("rya", n_low(s, keep_s), h, s, dy), r["rsr"].at[h, s], dev(z, yy, x, c))
         for dx in dxs:
             xx = at(x, dx, X)
-            copy(part.at[h, s, y, xx, high(s)], head("rxb", n_high(s), h, s, dx), r["rsr"].at[h, s], dev(z, y, xx, c))
+            copy(part.at[h, s, y, xx, high(s, keep_s)], head("rxb", n_high(s, keep_s), h, s, dx), r["rsr"].at[h, s], dev(z, y, xx, c))
 
     def rs2(h, s):
         if dxs and dys:
-            arrive(r["rsf"].at[h, s], len(dxs) * len(dys) * (n_low(s) + n_high(s)))
+            arrive(r["rsf"].at[h, s], len(dxs) * len(dys) * (n_low(s, keep_s) + n_high(s, keep_s)))
         for dx in dxs:
             xx = at(x, dx, X)
-            ref = part.at[h, s, y, xx, low(s)]
+            ref = part.at[h, s, y, xx, low(s, keep_s)]
             total = ref[...]
             for dy in dys:
-                total = total + head("rda", n_low(s), h, s, dy, dx)[...]
+                total = total + head("rda", n_low(s, keep_s), h, s, dy, dx)[...]
             ref[...] = total
-            copy(ref, head("rxa", n_low(s), h, s, dx), r["rsr"].at[h, s], dev(z, y, xx, c))
+            copy(ref, head("rxa", n_low(s, keep_s), h, s, dx), r["rsr"].at[h, s], dev(z, y, xx, c))
         for dy in dys:
             yy = at(y, dy, Y)
-            ref = part.at[h, s, yy, x, high(s)]
+            ref = part.at[h, s, yy, x, high(s, keep_s)]
             total = ref[...]
             for dx in dxs:
-                total = total + head("rdb", n_high(s), h, s, dy, dx)[...]
+                total = total + head("rdb", n_high(s, keep_s), h, s, dy, dx)[...]
             ref[...] = total
-            copy(ref, head("ryb", n_high(s), h, s, dy), r["rsr"].at[h, s], dev(z, yy, x, c))
+            copy(ref, head("ryb", n_high(s, keep_s), h, s, dy), r["rsr"].at[h, s], dev(z, yy, x, c))
 
     fin = r["fin"]
 
     def rs3(h, s):
         if dxs or dys:
-            arrive(r["rsr"].at[h, s], (len(dxs) + len(dys)) * (n_low(s) + n_high(s)))
-        total = part[h, s, y, x, low(s)]
+            arrive(r["rsr"].at[h, s], (len(dxs) + len(dys)) * (n_low(s, keep_s) + n_high(s, keep_s)))
+        total = part[h, s, y, x, low(s, keep_s)]
         for name, ds in (("rya", dys), ("rxa", dxs)):
             for d in ds:
-                total = total + head(name, n_low(s), h, s, d)[...]
-        fin[h, s, low(s)] = total
-        total = part[h, s, y, x, high(s)]
+                total = total + head(name, n_low(s, keep_s), h, s, d)[...]
+        fin[h, s, low(s, keep_s)] = total
+        total = part[h, s, y, x, high(s, keep_s)]
         for name, ds in (("rxb", dxs), ("ryb", dys)):
             for d in ds:
-                total = total + head(name, n_high(s), h, s, d)[...]
-        fin[h, s, high(s)] = total
-        if s == 1 and keep is not None:
+                total = total + head(name, n_high(s, keep_s), h, s, d)[...]
+        fin[h, s, high(s, keep_s)] = total
+        if s == 1 and keep_s is not None:
             fin[h, s, middle] = part[h, s, y, x, middle]
         if s:
             copy(fin.at[h, s], r["rz"].at[h, z], r["rsz"].at[h], dev(near(s), y, x, c))
@@ -606,7 +617,7 @@
 
     prepared = set()
     steps = dict(
-        ownp=send_own, ownz=to_plane, prep=prepare, zin=zin, diag=diag, share=share, fin=multiply, give=give,
+        ownp=send_own, ownz=to_plane, prep=prepare, zin=zin, ownq=in_plane_rest, zot=in_plane_rest, rst=rs_rest, diag=diag, share=share, fin=multiply, give=give,
         take=give_take, rs1=rs1, rs2=rs2, rs3=rs3, collect=collect, sum=lambda k, i: (gram, spectrum)[k][i](),
         panel=panel, finish=finish,
     )

time: 50.3 us -> 49 us (0.974)
  Pallas kernels: 49.5 us -> 48.2 us
    pallas_call x1, Pallas kernels: 48.4 us -> 47.1 us  [body(): pl.pallas_call(functools.partial(kernel, grid, total_pixels), out_shape=(...]
where the time goes in v4:
time: 49 us; the launch traced here: 48.9 us
  Pallas kernels  48.2 us (98%)
  between operations  0.64 us (1%)
    pallas_call x1, Pallas kernels, body(): pl.pallas_call(functools.partial(kernel, grid, total_pixels), out_shape=(...  47.1 us
    pallas_call x1, Pallas kernels, body(): pl.pallas_call(functools.partial(finish_kernel, patches), out_shape=(tall...  1.13 us

profile of v4, /device:TPU:0, one launch (start us, length us, event | category | flops | bytes accessed | tf_op | source)
XLA Modules:
  0.0 48.9 jit_solution(1162675069145974192)
XLA Ops:
  0.6 47.1 %shard_map.49 = (f32[64,128]{1,0:T(8,128)S(1)}, f32[192,128]{1,0:T(8,128)S(1)}, f32[128,128]{1,0:T(8,128)S(1)}, f32[128,128]{1,0:T(8,128)S(1)}) custom-call(f32[64,6144]{1,0:T(8,128)} %green_in.1, f32[192,128]{1,0:T(8,128)} %sketch_in.1), custom_call_target="tpu_custom_call" | custom-call | tf_op jit(solution)/shard_map/pallas_call | solution.py:683
  47.7 1.1 %shard_map.50 = (f32[64,128]{1,0:T(8,128)}, f32[192,128]{1,0:T(8,128)}, f32[128,128]{1,0:T(8,128)}) custom-call(f32[64,128]{1,0:T(8,128)S(1)} %get-tuple-element.7.basis_in, f32[192,128]{1,0:T(8,128)S(1)} %get-tuple-element.8.projection_in, f32[128,128]{1,0:T(8,128)S(1)} %get-tuple-element.9.inverse_in, f32[128,128]{1,0:T(8,128)S(1)} %get-tuple-element.10.spec_in), custom_call_target="tpu_custom_call" | custom-call | tf_op jit(solution)/shard_map/pallas_call | solution.py:693

commit v5 on v4

--- a/solution.py
+++ b/solution.py
@@ -56,7 +56,7 @@
         ("ownz", 1, 3), ("zin", 0, 2), ("ownz", 1, 2), ("zin", 0, 3), ("zot", 0, 2), ("zot", 0, 3),
         ("prep", 1), ("diag", 0, 1), ("zin", 1, 1), ("prep", 2), ("diag", 0, 2), ("prep", 0),
         ("diag", 0, 3), ("zin", 1, 2), ("zin", 1, 3), ("zot", 1, 1), ("zot", 1, 2), ("zot", 1, 3),
-        ("fin", 0, 1), ("fin", 0, 0), ("diag", 1, 1), ("fin", 0, 2), ("fin", 0, 3), ("give", 0),
+        ("fin", 0, 1), ("fin", 0, 0), ("fin", 0, 2), ("diag", 1, 1), ("fin", 0, 3), ("give", 0),
         ("diag", 1, 2), ("diag", 1, 3), ("take", 0), ("rs1", 0, 1), ("rs1", 0, 2), ("rst", 0, 2),
         ("rs1", 0, 3), ("fin", 1, 1), ("rst", 0, 1), ("fin", 1, 0), ("fin", 1, 2), ("rst", 0, 3),
         ("fin", 1, 3), ("give", 1), ("rs2", 0, 1), ("rs2", 0, 2), ("take", 1), ("rs1", 1, 3),

time: 49 us -> 49 us (level)
  no operation moved by 1% of the time
where the time goes in v5:
time: 49 us; the launch traced here: 48.8 us
  Pallas kernels  48.2 us (98%)
  between operations  0.64 us (1%)
    pallas_call x1, Pallas kernels, body(): pl.pallas_call(functools.partial(kernel, grid, total_pixels), out_shape=(...  47 us
    pallas_call x1, Pallas kernels, body(): pl.pallas_call(functools.partial(finish_kernel, patches), out_shape=(tall...  1.13 us

profile of v5, /device:TPU:0, one launch (start us, length us, event | category | flops | bytes accessed | tf_op | source)
XLA Modules:
  0.0 48.8 jit_solution(1273817900134105794)
XLA Ops:
  0.6 47.0 %shard_map.49 = (f32[64,128]{1,0:T(8,128)S(1)}, f32[192,128]{1,0:T(8,128)S(1)}, f32[128,128]{1,0:T(8,128)S(1)}, f32[128,128]{1,0:T(8,128)S(1)}) custom-call(f32[64,6144]{1,0:T(8,128)} %green_in.1, f32[192,128]{1,0:T(8,128)} %sketch_in.1), custom_call_target="tpu_custom_call" | custom-call | tf_op jit(solution)/shard_map/pallas_call | solution.py:683
  47.7 1.1 %shard_map.50 = (f32[64,128]{1,0:T(8,128)}, f32[192,128]{1,0:T(8,128)}, f32[128,128]{1,0:T(8,128)}) custom-call(f32[64,128]{1,0:T(8,128)S(1)} %get-tuple-element.7.basis_in, f32[192,128]{1,0:T(8,128)S(1)} %get-tuple-element.8.projection_in, f32[128,128]{1,0:T(8,128)S(1)} %get-tuple-element.9.inverse_in, f32[128,128]{1,0:T(8,128)S(1)} %get-tuple-element.10.spec_in), custom_call_target="tpu_custom_call" | custom-call | tf_op jit(solution)/shard_map/pallas_call | solution.py:693
